TPU v7x, 32 devices: a 4x4x1 block of a 4x4x8 slice. The times are simulated.
32 devices in a mesh: dp: 1 (over z), sp: 4 (over y), tp: 8 (over x, core).
Axes of the slice: x: 4, y: 4, z: 1, core: 2. Of those that a mesh axis runs over, the one named last changes fastest.
The devices are a block of a 4x4x8 slice.
Arguments:
- hidden: bfloat16 [256, 3072], P('dp')
- new_pos: int32 [256], P('dp')
- k_self: bfloat16 [256, 256, 8, 128], P('dp', 'sp', 'tp')
- v_self: bfloat16 [256, 256, 8, 128], P('dp', 'sp', 'tp')
- k_cross: bfloat16 [256, 512, 8, 128], P('dp', None, 'tp')
- v_cross: bfloat16 [256, 512, 8, 128], P('dp', None, 'tp')
- xvalid: int32 [256, 512], P('dp')
- rowmask: int32 [256], P('dp')
- self_attn_norm: bfloat16 [3072], replicated
- self_wq: bfloat16 [3072, 3072], P(None, 'tp')
- self_wk: bfloat16 [3072, 1024], P(None, 'tp')
- self_wv: bfloat16 [3072, 1024], P(None, 'tp')
- self_wo: bfloat16 [3072, 3072], P('tp')
- self_mlp_norm: bfloat16 [3072], replicated
- self_wgate: bfloat16 [3072, 8192], P(None, 'tp')
- self_wup: bfloat16 [3072, 8192], P(None, 'tp')
- self_wdown: bfloat16 [8192, 3072], P('tp')
- cross_attn_norm: bfloat16 [3072], replicated
- cross_wq: bfloat16 [3072, 3072], P(None, 'tp')
- cross_qnorm: bfloat16 [128], replicated
- cross_wo: bfloat16 [3072, 3072], P('tp')
- cross_gates: float32 [2], replicated
- cross_mlp_norm: bfloat16 [3072], replicated
- cross_wgate: bfloat16 [3072, 8192], P(None, 'tp')
- cross_wup: bfloat16 [3072, 8192], P(None, 'tp')
- cross_wdown: bfloat16 [8192, 3072], P('tp')
Outputs:
- output 1: bfloat16 [256, 3072], P('dp')
- output 2: bfloat16 [256, 256, 8, 128], P('dp', 'sp', 'tp')
- output 3: bfloat16 [256, 256, 8, 128], P('dp', 'sp', 'tp')
All inputs are finite; a program needn't handle non-finite values.
Results may differ from a plain program's by a relative error of at most 0.0147007.
Values sent between devices are 32-bit elements.
A program may use at most 768 MiB of HBM per device.

v0:
```python
import math
import jax
import jax.numpy as jnp
from jax import lax
from jax.sharding import PartitionSpec as P

NORM_EPS = 1e-5
ROPE_THETA = 500000.0
ROPE_FACTOR = 8.0
LOW_FREQ = 1.0
HIGH_FREQ = 4.0
ORIG_CTX = 8192.0
NEG_BIG = -1e30


def rope_freqs(head_dim):
    inv_freq = 1.0 / (ROPE_THETA ** (jnp.arange(0, head_dim, 2).astype(jnp.float32) / head_dim))
    wavelen = 2.0 * math.pi / inv_freq
    smooth = (ORIG_CTX / wavelen - LOW_FREQ) / (HIGH_FREQ - LOW_FREQ)
    mid_freq = (1.0 - smooth) * inv_freq / ROPE_FACTOR + smooth * inv_freq
    scaled = jnp.where(wavelen > ORIG_CTX / LOW_FREQ, inv_freq / ROPE_FACTOR, mid_freq)
    return jnp.where(wavelen < ORIG_CTX / HIGH_FREQ, inv_freq, scaled)


def apply_rope(vectors, positions):
    head_dim = vectors.shape[-1]
    half_dim = head_dim // 2
    angles = positions.astype(jnp.float32)[:, None] * rope_freqs(head_dim)[None, :]
    cos_t = jnp.cos(angles)[:, None, :]
    sin_t = jnp.sin(angles)[:, None, :]
    first_half = vectors[..., :half_dim]
    second_half = vectors[..., half_dim:]
    return jnp.concatenate([first_half * cos_t - second_half * sin_t, second_half * cos_t + first_half * sin_t], axis=-1)


def rms_norm(values, gain_vec):
    vals32 = values.astype(jnp.float32)
    inv_rms = lax.rsqrt(jnp.mean(vals32 * vals32, axis=-1, keepdims=True) + NORM_EPS)
    return (vals32 * inv_rms * gain_vec.astype(jnp.float32)).astype(jnp.bfloat16)


def mlp_partial(normed, w_gate, w_up, w_down):
    gate_val = jnp.dot(normed, w_gate, preferred_element_type=jnp.float32).astype(jnp.bfloat16)
    up_val = jnp.dot(normed, w_up, preferred_element_type=jnp.float32).astype(jnp.bfloat16)
    hidden_act = (jax.nn.silu(gate_val.astype(jnp.float32)) * up_val.astype(jnp.float32)).astype(jnp.bfloat16)
    return jnp.dot(hidden_act, w_down, preferred_element_type=jnp.float32)


def local_softmax(queries, key_rows, val_rows, valid_mask, score_scale):
    scores = jnp.einsum('bkgd,btkd->bkgt', queries, key_rows, preferred_element_type=jnp.float32) * score_scale
    scores = jnp.where(valid_mask, scores, NEG_BIG)
    part_max = jnp.max(scores, axis=-1)
    probs_loc = jnp.where(valid_mask, jnp.exp(scores - part_max[..., None]), 0.0)
    part_sum = jnp.sum(probs_loc, axis=-1)
    part_out = jnp.einsum('bkgt,btkd->bkgd', probs_loc.astype(jnp.bfloat16), val_rows, preferred_element_type=jnp.float32)
    return part_max, part_sum, part_out


def combine_sp(part_max, part_sum, part_out):
    glob_max = lax.pmax(part_max, 'sp')
    factor = jnp.exp(part_max - glob_max)
    total_sum = lax.psum(part_sum * factor, 'sp')
    total_out = lax.psum(part_out * factor[..., None], 'sp')
    return total_out / total_sum[..., None]


def solution(mesh):
    cache_spec = P('dp', 'sp', 'tp', None)
    cross_spec = P('dp', None, 'tp', None)
    row_spec = P('dp', None)
    vec_spec = P('dp')
    full_spec = P(None)
    col_spec = P(None, 'tp')
    split_rows = P('tp', None)
    in_specs = (row_spec, vec_spec, cache_spec, cache_spec, cross_spec, cross_spec, row_spec, vec_spec,
                full_spec, col_spec, col_spec, col_spec, split_rows, full_spec, col_spec, col_spec, split_rows,
                full_spec, col_spec, full_spec, split_rows, full_spec, full_spec, col_spec, col_spec, split_rows)
    out_specs = (row_spec, cache_spec, cache_spec)

    def local_step(hidden, new_pos, k_self, v_self, k_cross, v_cross, xvalid, rowmask,
                   self_attn_norm, self_wq, self_wk, self_wv, self_wo, self_mlp_norm,
                   self_wgate, self_wup, self_wdown, cross_attn_norm, cross_wq, cross_qnorm,
                   cross_wo, cross_gates, cross_mlp_norm, cross_wgate, cross_wup, cross_wdown):
        batch_rows = hidden.shape[0]
        len_local = k_self.shape[1]
        kv_local = k_self.shape[2]
        head_dim = k_self.shape[3]
        heads_local = self_wq.shape[1] // head_dim
        group_size = heads_local // kv_local
        score_scale = head_dim ** -0.5
        normed = rms_norm(hidden, self_attn_norm)
        queries = jnp.dot(normed, self_wq, preferred_element_type=jnp.float32).astype(jnp.bfloat16)
        key_new = jnp.dot(normed, self_wk, preferred_element_type=jnp.float32).astype(jnp.bfloat16)
        val_new = jnp.dot(normed, self_wv, preferred_element_type=jnp.float32).astype(jnp.bfloat16)
        queries = apply_rope(queries.reshape(batch_rows, heads_local, head_dim).astype(jnp.float32), new_pos).astype(jnp.bfloat16)
        key_new = apply_rope(key_new.reshape(batch_rows, kv_local, head_dim).astype(jnp.float32), new_pos).astype(jnp.bfloat16)
        val_new = val_new.reshape(batch_rows, kv_local, head_dim)
        local_pos = new_pos - lax.axis_index('sp') * len_local
        slot_ids = jnp.arange(len_local)
        hit_mask = (slot_ids[None, :] == local_pos[:, None])[:, :, None, None]
        k_new_cache = jnp.where(hit_mask, key_new[:, None], k_self)
        v_new_cache = jnp.where(hit_mask, val_new[:, None], v_self)
        seen_mask = (slot_ids[None, :] <= local_pos[:, None])[:, None, None, :]
        self_stats = local_softmax(queries.reshape(batch_rows, kv_local, group_size, head_dim), k_new_cache, v_new_cache, seen_mask, score_scale)
        self_attn = combine_sp(self_stats[0], self_stats[1], self_stats[2])
        self_flat = self_attn.astype(jnp.bfloat16).reshape(batch_rows, heads_local * head_dim)
        attn_sum = lax.psum(jnp.dot(self_flat, self_wo, preferred_element_type=jnp.float32), 'tp')
        after_attn = (hidden.astype(jnp.float32) + attn_sum).astype(jnp.bfloat16)
        mlp_sum = lax.psum(mlp_partial(rms_norm(after_attn, self_mlp_norm), self_wgate, self_wup, self_wdown), 'tp')
        after_mlp = (after_attn.astype(jnp.float32) + mlp_sum).astype(jnp.bfloat16)
        normed = rms_norm(after_mlp, cross_attn_norm)
        cross_q = jnp.dot(normed, cross_wq, preferred_element_type=jnp.float32).astype(jnp.bfloat16)
        cross_q = rms_norm(cross_q.reshape(batch_rows, heads_local, head_dim), cross_qnorm)
        cross_mask = (xvalid > 0)[:, None, None, :]
        cross_stats = local_softmax(cross_q.reshape(batch_rows, kv_local, group_size, head_dim), k_cross, v_cross, cross_mask, score_scale)
        cross_attn = cross_stats[2] / cross_stats[1][..., None]
        cross_flat = cross_attn.astype(jnp.bfloat16).reshape(batch_rows, heads_local * head_dim)
        gate_vals = jnp.tanh(cross_gates.astype(jnp.float32))
        row_scale = rowmask.astype(jnp.float32)[:, None]
        xattn_sum = lax.psum(jnp.dot(cross_flat, cross_wo, preferred_element_type=jnp.float32), 'tp')
        after_cross = (after_mlp.astype(jnp.float32) + gate_vals[0] * row_scale * xattn_sum).astype(jnp.bfloat16)
        xmlp_sum = lax.psum(mlp_partial(rms_norm(after_cross, cross_mlp_norm), cross_wgate, cross_wup, cross_wdown), 'tp')
        after_xmlp = (after_cross.astype(jnp.float32) + gate_vals[1] * row_scale * xmlp_sum).astype(jnp.bfloat16)
        return after_xmlp, k_new_cache, v_new_cache

    return jax.shard_map(local_step, mesh=mesh, in_specs=in_specs, out_specs=out_specs, check_vma=False)
```

profile of v0, /device:TPU:97, one launch (start us, length us, event | category | flops | bytes accessed | tf_op | source)
XLA Modules:
  0.0 445.9 jit_solution(13029736362565039648)
XLA Ops:
  8.2 1.8 fusion.9
  10.8 1.2 multiply_cosine_fusion
  12.0 2.4 fusion.62
  15.4 2.8 convolution_convert_fusion.5
  19.0 2.7 fusion.45
  22.8 1.2 copy.39
  24.0 1.2 subtract_convert_fusion
  25.2 8.5 %broadcast_select_fusion.1 = (bf16[256,64,1,128]{3,1,2,0:T(8,128)(2,1)S(1)}, bf16[256,64,1,128]{3,1,2,0:T(8,128)(2,1)}) fusion(bf16[256,64,1,128]{3,1,2,0:T(8,128)(2,1)} %param.28, pred[256,64]{1,0:T(8,128)(4,1)} %get-tuple-element.24, bf16[256,128]{1,0:T(8,128)(2,1)} %copy.33, bf16[256,64,1,128]{3,1,2,0:T(8,128)(2,1)} %param.29, ...), kind=kLoop, calls=%fused_computation.22 | loop fusion | flops 4194304 | bytes 16924672 | tf_op jit(solution)/shard_map/jit(_where)/select_n | solution.py:101
  33.7 2.0 copy-done.2
  35.7 2.4 fusion.115
  38.9 17.4 %pmax.7 = f32[256,1,3]{2,0,1:T(8,128)S(1)} all-reduce(f32[256,1,3]{2,0,1:T(8,128)S(1)} %bitcast.76), channel_id=1, replica_groups=mesh['dp'=1,'sp'=4,'tp'=8] {'sp'}, use_global_device_ids=true, to_apply=%region_2.3 | all-reduce | flops 768 | bytes 6144 | tf_op jit(solution)/shard_map/pmax | solution.py:60
  56.3 4.3 fusion.42
  60.7 12.6 %psum.43 = f32[256,3]{1,0:T(8,128)S(1)} all-reduce(f32[256,3]{1,0:T(8,128)S(1)} %get-tuple-element.13), channel_id=1, replica_groups=mesh['dp'=1,'sp'=4,'tp'=8] {'sp'}, use_global_device_ids=true, to_apply=%region_5.6 | all-reduce | flops 768 | bytes 6144 | tf_op jit(solution)/shard_map/psum | solution.py:62
  73.3 27.4 %all-reduce.6.cloned.1.call-done = f32[256,1,3,128]{3,2,0,1:T(4,128)} async-done(((f32[256,1,3,128]{3,2,0,1:T(4,128)}), f32[256,1,3,128]{3,2,0,1:T(4,128)}) %all-reduce.6.cloned.1.call-update) | async-done | bytes 393232 | tf_op jit(solution)/shard_map/psum | solution.py:63
  100.7 1.4 divide_convert_fusion
  102.3 2.7 fusion.121
  105.3 64.4 %all-reduce.8.cloned.1.call-done = f32[256,3072]{1,0:T(8,128)} async-done(((f32[256,3072]{1,0:T(8,128)}), f32[256,3072]{1,0:T(8,128)}) %all-reduce.8.cloned.1.call-update) | async-done | bytes 3145744 | tf_op jit(solution)/shard_map/psum | solution.py:107
  169.7 2.5 fusion.13
  173.4 4.7 %convert_multiply_fusion.9 = f32[256,1024]{1,0:T(8,128)S(1)} fusion(bf16[3072,1024]{1,0:T(8,128)(2,1)} %param.40, bf16[256,3072]{1,0:T(8,128)(2,1)S(1)} %get-tuple-element.8, f32[3072]{0:T(1024)S(1)} %convert_element_type.180, f32[256]{0:T(256)S(1)} %add_rsqrt_fusion.3), kind=kOutput, calls=%fused_computation.47 | convolution fusion | flops 1615331328 | bytes 8926208 | tf_op jit(solution)/shard_map/dot_general | solution.py:43
  178.1 10.2 %fusion.74 = f32[256,3072]{1,0:T(8,128)} fusion(bf16[1024,3072]{1,0:T(8,128)(2,1)} %param.42, f32[256,1024]{1,0:T(8,128)S(1)} %convert_multiply_fusion.9, bf16[3072,1024]{1,0:T(8,128)(2,1)} %param.41, bf16[256,3072]{1,0:T(8,128)(2,1)} %copy-done.6, f32[3072]{0:T(1024)S(1)} %convert_element_type.180, f32[256]{0:T(256)S(1)} %add_rsqrt_fusion.3), kind=kOutput, calls=%fused_computation.84 | convolution fusion | flops 3225419776 | bytes 18363392 | tf_op jit(solution)/shard_map/dot_general | solution.py:46
  189.5 62.6 %all-reduce.10.cloned.1.call-done = f32[256,3072]{1,0:T(8,128)} async-done(((f32[256,3072]{1,0:T(8,128)}), f32[256,3072]{1,0:T(8,128)}) %all-reduce.10.cloned.1.call-update) | async-done | bytes 3145744 | tf_op jit(solution)/shard_map/psum | solution.py:109
  252.0 3.1 fusion.17
  256.8 14.8 %fusion.116 = (f32[256,3]{1,0:T(8,128)S(1)}, bf16[256,3,512]{2,1,0:T(4,128)(2,1)S(1)}) fusion(pred[256,512]{1,0:T(8,128)(4,1)S(1)} %broadcast_compare_fusion, bf16[256,3,128]{2,1,0:T(4,128)(2,1)S(1)} %copy.36, bf16[256,512,1,128]{3,1,2,0:T(8,128)(2,1)} %param.30), kind=kOutput, calls=%fused_computation.139 | convolution fusion | flops 103023104 | bytes 34671616 | tf_op jit(solution)/shard_map/sub | solution.py:53
  271.6 12.8 %fusion.58 = bf16[256,3,128]{2,1,0:T(4,128)(2,1)S(1)} fusion(bf16[256,512,1,128]{3,1,2,0:T(8,128)(2,1)} %param.31, bf16[256,3,512]{2,1,0:T(4,128)(2,1)S(1)} %get-tuple-element.32, f32[256,3]{1,0:T(8,128)S(1)} %get-tuple-element.31), kind=kOutput, calls=%fused_computation.68 | convolution fusion | flops 100859904 | bytes 34540544 | tf_op jit(solution)/shard_map/bkgt,btkd->bkgd/dot_general | solution.py:55
  284.6 4.4 fusion.122
  290.0 1.2 convert_multiply_fusion.10
  291.2 61.5 %all-reduce.12.cloned.1.call-done = f32[256,3072]{1,0:T(8,128)} async-done(((f32[256,3072]{1,0:T(8,128)}), f32[256,3072]{1,0:T(8,128)}) %all-reduce.12.cloned.1.call-update) | async-done | bytes 3145744 | tf_op jit(solution)/shard_map/psum | solution.py:120
  352.7 2.6 fusion.21
  356.5 4.7 %convert_multiply_fusion.8 = f32[256,1024]{1,0:T(8,128)S(1)} fusion(bf16[3072,1024]{1,0:T(8,128)(2,1)} %param.49, bf16[256,3072]{1,0:T(8,128)(2,1)S(1)} %get-tuple-element.4, f32[3072]{0:T(1024)S(1)} %convert_element_type.201, f32[256]{0:T(256)S(1)} %add_rsqrt_fusion.1), kind=kOutput, calls=%fused_computation.45 | convolution fusion | flops 1615331328 | bytes 8926208 | tf_op jit(solution)/shard_map/dot_general | solution.py:43
  361.2 10.2 %fusion.73 = f32[256,3072]{1,0:T(8,128)} fusion(bf16[1024,3072]{1,0:T(8,128)(2,1)} %param.51, f32[256,1024]{1,0:T(8,128)S(1)} %convert_multiply_fusion.8, bf16[3072,1024]{1,0:T(8,128)(2,1)} %param.50, bf16[256,3072]{1,0:T(8,128)(2,1)} %copy-done.5, f32[3072]{0:T(1024)S(1)} %convert_element_type.201, f32[256]{0:T(256)S(1)} %add_rsqrt_fusion.1), kind=kOutput, calls=%fused_computation.83 | convolution fusion | flops 3225419776 | bytes 18363392 | tf_op jit(solution)/shard_map/dot_general | solution.py:46
  371.5 63.6 %all-reduce.14.cloned.1.call-done = f32[256,3072]{1,0:T(8,128)} async-done(((f32[256,3072]{1,0:T(8,128)}), f32[256,3072]{1,0:T(8,128)}) %all-reduce.14.cloned.1.call-update) | async-done | bytes 3145744 | tf_op jit(solution)/shard_map/psum | solution.py:122
  435.1 4.2 fusion.24
  (74 shorter events, 12.2 us)
Async XLA Ops:
  7.2 95.1 %copy-start = (bf16[384,3072]{1,0:T(8,128)(2,1)S(1)}, bf16[384,3072]{1,0:T(8,128)(2,1)}, u32[]{:S(2)}) copy-start(bf16[384,3072]{1,0:T(8,128)(2,1)} %param.38) | copy-start | bytes 7077892
  7.2 8.2 %copy-start.14 = (bf16[3072,128]{1,0:T(8,128)(2,1)S(1)}, bf16[3072,128]{1,0:T(8,128)(2,1)}, u32[]{:S(2)}) copy-start(bf16[3072,128]{1,0:T(8,128)(2,1)} %param.37) | copy-start | bytes 2359300
  7.2 93.5 %all-reduce.6.cloned.1.call-start = ((), (), s32[]{:S(2)}) async-start(), calls=%async_computation | async-start | bytes 1048576 | tf_op jit(solution)/shard_map/psum | solution.py:63
  15.4 3.6 copy-start.3
  25.1 10.6 %copy-start.8 = (pred[256,64]{1,0:T(8,128)(4,1)S(1)}, pred[256,64]{1,0:T(8,128)(4,1)}, u32[]{:S(2)}) copy-start(pred[256,64]{1,0:T(8,128)(4,1)} %get-tuple-element.23) | copy-start | bytes 49156
  33.7 2.0 copy-start.2
  60.6 109.1 %all-reduce.8.cloned.1.call-start = ((), (), s32[]{:S(2)}) async-start(), calls=%async_computation.1 | async-start | bytes 6291456 | tf_op jit(solution)/shard_map/psum | solution.py:107
  102.3 3.0 copy-start.9
  105.0 64.7 %copy-start.4 = (bf16[256,3072]{1,0:T(8,128)(2,1)S(1)}, bf16[256,3072]{1,0:T(8,128)(2,1)}, u32[]{:S(2)}) copy-start(bf16[256,3072]{1,0:T(8,128)(2,1)} %param.26) | copy-start | bytes 4718596
  105.1 147.0 %all-reduce.10.cloned.1.call-start = ((), (), s32[]{:S(2)}) async-start(), calls=%async_computation.2 | async-start | bytes 6291456 | tf_op jit(solution)/shard_map/psum | solution.py:109
  172.2 1.1 copy-start.6
  188.3 0.7 copy-start.10
  188.3 0.7 copy-start.15
  188.3 1.1 copy-start.7
  188.4 164.3 %all-reduce.12.cloned.1.call-start = ((), (), s32[]{:S(2)}) async-start(), calls=%async_computation.3 | async-start | bytes 6291456 | tf_op jit(solution)/shard_map/psum | solution.py:120
  252.0 3.1 copy-start.13
  284.6 4.8 %copy-start.16 = (f32[2]{0:T(128)S(1)}, f32[2]{0:T(128)}, u32[]{:S(2)}) copy-start(f32[2]{0:T(128)} %param.47) | copy-start | bytes 28
  284.6 4.8 %copy-start.11 = (bf16[3072]{0:T(1024)(128)(2,1)S(1)}, bf16[3072]{0:T(1024)(128)(2,1)}, u32[]{:S(2)}) copy-start(bf16[3072]{0:T(1024)(128)(2,1)} %param.48) | copy-start | bytes 18436
  284.6 5.4 %copy-start.12 = (s32[256]{0:T(256)S(1)}, s32[256]{0:T(256)}, u32[]{:S(2)}) copy-start(s32[256]{0:T(256)} %param.33) | copy-start | bytes 3076
  289.1 146.0 %all-reduce.14.cloned.1.call-start = ((), (), s32[]{:S(2)}) async-start(), calls=%async_computation.4 | async-start | bytes 6291456 | tf_op jit(solution)/shard_map/psum | solution.py:122
  355.3 1.1 copy-start.5
  435.1 4.2 copy-start.1
Sparse Core Ops, SparseCore 0:
  60.7 39.9 all-reduce.5
  105.2 64.4 all-reduce.7
  188.5 63.4 all-reduce.9
  289.2 63.4 all-reduce.11
  371.6 63.4 all-reduce.13
where the time goes:
time: 447 us; the launch traced here: 446 us
  waiting for transfers between devices  280 us (63%)
  matrix products  80.3 us (18%)
  other arithmetic  31.5 us (7%)
  blocking collectives  29.9 us (7%)
  between operations  14.2 us (3%)
  local copies, waits for them, and re-layouts  9.52 us (2%)
    psum x1, waiting for transfers between devices, local_step(): lax.psum(jnp.dot(self_flat, self_wo, preferred_element_type=jnp.float32),...  64.4 us
    psum x1, waiting for transfers between devices, local_step(): lax.psum(mlp_partial(rms_norm(after_cross, cross_mlp_norm), cross_wgate,...  63.6 us
    psum x1, waiting for transfers between devices, local_step(): lax.psum(mlp_partial(rms_norm(after_attn, self_mlp_norm), self_wgate, sel...  62.6 us
    psum x1, waiting for transfers between devices, local_step(): lax.psum(jnp.dot(cross_flat, cross_wo, preferred_element_type=jnp.float32...  61.5 us
    psum x1, waiting for transfers between devices, combine_sp(): total_out = lax.psum(part_out * factor[..., None], 'sp')  27.4 us
    dot_general x2, matrix products, mlp_partial(): return jnp.dot(hidden_act, w_down, preferred_element_type=jnp.float32)  20.5 us
    pmax x1, blocking collectives, combine_sp(): glob_max = lax.pmax(part_max, 'sp')  17.4 us
    dot_general x2, matrix products, local_softmax(): jnp.einsum('bkgt,btkd->bkgd', probs_loc.astype(jnp.bfloat16), val_rows, p...  17.1 us
  transfers between devices with their start and end apart: 5, of which 5 were waited for; matrix products, arithmetic and copies ran while one was open for 0% of the time, Pallas kernels for 0%

commit v1 on v0

--- a/solution.py
+++ b/solution.py
@@ -1,7 +1,10 @@
+import functools
 import math
 import jax
 import jax.numpy as jnp
 from jax import lax
+from jax.experimental import pallas as pl
+from jax.experimental.pallas import tpu as pltpu
 from jax.sharding import PartitionSpec as P
 
 NORM_EPS = 1e-5
@@ -11,6 +14,8 @@
 HIGH_FREQ = 4.0
 ORIG_CTX = 8192.0
 NEG_BIG = -1e30
+NC = 4
+MESH = pl.DeviceIdType.MESH
 
 
 def rope_freqs(head_dim):
@@ -39,13 +44,6 @@
     return (vals32 * inv_rms * gain_vec.astype(jnp.float32)).astype(jnp.bfloat16)
 
 
-def mlp_partial(normed, w_gate, w_up, w_down):
-    gate_val = jnp.dot(normed, w_gate, preferred_element_type=jnp.float32).astype(jnp.bfloat16)
-    up_val = jnp.dot(normed, w_up, preferred_element_type=jnp.float32).astype(jnp.bfloat16)
-    hidden_act = (jax.nn.silu(gate_val.astype(jnp.float32)) * up_val.astype(jnp.float32)).astype(jnp.bfloat16)
-    return jnp.dot(hidden_act, w_down, preferred_element_type=jnp.float32)
-
-
 def local_softmax(queries, key_rows, val_rows, valid_mask, score_scale):
     scores = jnp.einsum('bkgd,btkd->bkgt', queries, key_rows, preferred_element_type=jnp.float32) * score_scale
     scores = jnp.where(valid_mask, scores, NEG_BIG)
@@ -56,12 +54,514 @@
     return part_max, part_sum, part_out
 
 
-def combine_sp(part_max, part_sum, part_out):
-    glob_max = lax.pmax(part_max, 'sp')
-    factor = jnp.exp(part_max - glob_max)
-    total_sum = lax.psum(part_sum * factor, 'sp')
-    total_out = lax.psum(part_out * factor[..., None], 'sp')
-    return total_out / total_sum[..., None]
+def fdot(a, b):
+    return jnp.dot(a, b, preferred_element_type=jnp.float32)
+
+
+def tail_kernel(cfg, blk_h, hid_h, gains_v, rowm_v, gate_s, xv_h, kc_h, vc_h,
+                wo_h, wg_h, wu_h, wd_h, cq_h, cwo_h, cg_h, cu_h, cd_h, out_v,
+                bk, yr, yd, yt, yf, ob, hrow, hst,
+                wo_v, wg_v, wu_v, wd_v, cq_v, cwo_v, kc_v, vc_v, xv_v,
+                pbuf, dbuf, sbuf, rbuf, ebuf, tbuf, fbuf, xa, og, acc, act, q3, oc,
+                ld_sem, w_sem, kv_sem, ys, yrs, rs_s, rs_r, ag_s, ag_r, fg_s, fg_r):
+    heads, hd, dim, mlp, ntok = cfg
+    cw = dim // NC
+    hw = heads * hd
+    half = 32
+    x = lax.axis_index('tp') // 2
+    c = lax.axis_index('tp') % 2
+    y = lax.axis_index('sp')
+    slot = c * 4 + x
+    scale = hd ** -0.5
+
+    def ring(v):
+        return lax.rem(v + 8, 4)
+
+    def xdev(d):
+        return {'tp': 2 * ring(x + d) + c}
+
+    def ydev(d):
+        return {'sp': ring(y + d)}
+
+    sib = {'tp': 2 * x + 1 - c}
+
+    def rcopy(src, dst, ss, rs, dev):
+        return pltpu.make_async_remote_copy(src_ref=src, dst_ref=dst, send_sem=ss, recv_sem=rs,
+                                            device_id=dev, device_id_type=MESH)
+
+    def loop(n, body):
+        def step(i, carry):
+            body(i)
+            return carry
+        lax.fori_loop(0, n, step, 0)
+
+    blk_cp = pltpu.make_async_copy(blk_h, bk, ld_sem.at[0])
+    hid_cp = pltpu.make_async_copy(hid_h.at[y * 8 + slot], hrow, ld_sem.at[1])
+    xv_cp = pltpu.make_async_copy(xv_h.at[y], xv_v, ld_sem.at[2])
+
+    def cols(h, v, k, j):
+        return pltpu.make_async_copy(h.at[:, pl.ds(pl.multiple_of(j * cw, 128), cw)], v.at[j], w_sem.at[k, j])
+
+    def rows(h, v, k, j):
+        return pltpu.make_async_copy(h.at[pl.ds(pl.multiple_of(j * cw, 128), cw)], v.at[j], w_sem.at[k, j])
+
+    def ld_wo(j):
+        return cols(wo_h, wo_v, 0, j)
+
+    def ld_wg(j):
+        return rows(wg_h, wg_v, 1, j)
+
+    def ld_wu(j):
+        return rows(wu_h, wu_v, 2, j)
+
+    def ld_wd(j):
+        return cols(wd_h, wd_v, 3, j)
+
+    def ld_cq(j):
+        return rows(cq_h, cq_v, 4, j)
+
+    def ld_cwo(j):
+        return cols(cwo_h, cwo_v, 5, j)
+
+    def ld_cg(j):
+        return rows(cg_h, wg_v, 6, j)
+
+    def ld_cu(j):
+        return rows(cu_h, wu_v, 7, j)
+
+    def ld_cd(j):
+        return cols(cd_h, wd_v, 8, j)
+
+    def ld_kc(g):
+        return pltpu.make_async_copy(kc_h.at[y, pl.ds(g * 8, 8)], kc_v.at[pl.ds(g * 8, 8)], kv_sem.at[0, g])
+
+    def ld_vc(g):
+        return pltpu.make_async_copy(vc_h.at[y, pl.ds(g * 8, 8)], vc_v.at[pl.ds(g * 8, 8)], kv_sem.at[1, g])
+
+    blk_cp.start()
+    hid_cp.start()
+    xv_cp.start()
+    loop(NC, lambda j: ld_wo(j).start())
+
+    barrier = pltpu.get_barrier_semaphore()
+    for dev in (sib, xdev(1), xdev(-1), ydev(1), ydev(-1)):
+        pl.semaphore_signal(barrier, inc=1, device_id=dev, device_id_type=MESH)
+
+    def start_gu(j):
+        ld_wg(j).start()
+        ld_wu(j).start()
+
+    loop(NC, start_gu)
+    loop(NC, lambda j: ld_wd(j).start())
+    loop(NC, lambda j: ld_cq(j).start())
+
+    def start_kv(g):
+        ld_kc(g).start()
+        ld_vc(g).start()
+
+    loop(8, start_kv)
+    loop(NC, lambda j: ld_cwo(j).start())
+    q3[...] = jnp.zeros_like(q3)
+    pl.semaphore_wait(barrier, 5)
+
+    lane = lax.broadcasted_iota(jnp.int32, (half, hd), 1)
+
+    def merge(a, b):
+        outs, ms, ls = [], [], []
+        for h in range(heads):
+            ma, mb = a[:, hw + h:hw + h + 1], b[:, hw + h:hw + h + 1]
+            la, lb = a[:, hw + 8 + h:hw + 9 + h], b[:, hw + 8 + h:hw + 9 + h]
+            mm = jnp.maximum(ma, mb)
+            ea, eb = jnp.exp(ma - mm), jnp.exp(mb - mm)
+            outs.append(a[:, h * hd:(h + 1) * hd] * ea + b[:, h * hd:(h + 1) * hd] * eb)
+            ms.append(mm)
+            ls.append(la * ea + lb * eb)
+        stat = jnp.zeros((half, hd), jnp.float32)
+        for h in range(heads):
+            stat = jnp.where(lane == h, ms[h], stat)
+            stat = jnp.where(lane == 8 + h, ls[h], stat)
+        return jnp.concatenate(outs + [stat], axis=1), ls
+
+    def y_relay(j, d):
+        return rcopy(bk.at[ring(y + 2), j], yr.at[j], ys.at[0, j], yrs.at[0, j], ydev(d))
+
+    def y_direct(j, d):
+        return rcopy(bk.at[ring(y - d), j], yd.at[j], ys.at[1, j], yrs.at[1, j], ydev(-d))
+
+    def y_final(j, d):
+        return rcopy(yt.at[j], yf.at[j], ys.at[2, j], yrs.at[2, j], ydev(d))
+
+    blk_cp.wait()
+    for j, d in ((0, 1), (1, -1)):
+        y_relay(j, d).start()
+    for j, d in ((0, 1), (1, -1)):
+        y_direct(j, d).start()
+    for j, d in ((0, 1), (1, -1)):
+        y_relay(j, d).wait_recv()
+        yt[j] = merge(bk[ring(y + d), j], yr[j])[0]
+        y_final(j, d).start()
+    for j, d in ((0, 1), (1, -1)):
+        y_direct(j, d).wait_recv()
+        first = merge(bk[y, j], yd[j])[0]
+        y_final(j, d).wait_recv()
+        both, sums = merge(first, yf[j])
+        for h in range(heads):
+            ob[j * half:(j + 1) * half, h * hd:(h + 1) * hd] = (both[:, h * hd:(h + 1) * hd] / sums[h]).astype(jnp.bfloat16)
+
+    def rs_pair(p, j):
+        return rcopy(pbuf.at[p, j, 1 - c], dbuf.at[p, j], rs_s.at[p, 0, j], rs_r.at[p, 0, j], sib)
+
+    def turn(j):
+        return 1 - 2 * lax.rem(j, 2)
+
+    def rs_relay(p, j):
+        return rcopy(sbuf.at[p, j, ring(x + 2)], rbuf.at[p, j], rs_s.at[p, 1, j], rs_r.at[p, 1, j], xdev(turn(j)))
+
+    def rs_direct(p, j):
+        return rcopy(sbuf.at[p, j, ring(x - turn(j))], ebuf.at[p, j], rs_s.at[p, 2, j], rs_r.at[p, 2, j], xdev(-turn(j)))
+
+    def rs_final(p, j):
+        return rcopy(tbuf.at[p, j], fbuf.at[p, j], rs_s.at[p, 3, j], rs_r.at[p, 3, j], xdev(turn(j)))
+
+    def reduce_scatter(p, partial):
+        def second(j):
+            rs_pair(p, j).wait_recv()
+            sbuf[p, j] = (pbuf[p, j, c] + dbuf[p, j]).reshape(4, 8, cw)
+            rs_relay(p, j).start()
+            rs_direct(p, j).start()
+
+        def body(j):
+            @pl.when(j < NC)
+            def _():
+                pbuf[p, j] = partial(j).reshape(2, half, cw)
+                rs_pair(p, j).start()
+
+            @pl.when(j >= 1)
+            def _():
+                second(j - 1)
+
+        loop(NC + 1, body)
+
+        def third(j):
+            rs_relay(p, j).wait_recv()
+            tbuf[p, j] = sbuf[p, j, ring(x + turn(j))] + rbuf[p, j]
+            rs_final(p, j).start()
+
+        loop(NC, third)
+
+    def reduced(p, j):
+        rs_direct(p, j).wait_recv()
+        rs_final(p, j).wait_recv()
+        return sbuf[p, j, x] + ebuf[p, j] + fbuf[p, j]
+
+    def new_rows(p, factor):
+        sq = jnp.zeros((8, 1), jnp.float32)
+        for j in range(NC):
+            add = reduced(p, j)
+            if factor is not None:
+                add = factor * add
+            old = hrow[:, j * cw:(j + 1) * cw].astype(jnp.float32) if p == 0 else hst[j]
+            new = (old + add).astype(jnp.bfloat16).astype(jnp.float32)
+            hst[j] = new
+            sq = sq + jnp.sum(new * new, axis=1, keepdims=True)
+        return sq
+
+    def ag_send(q, j, s, k, dev):
+        return rcopy(xa.at[q, j, s], xa.at[q, j, s], ag_s.at[q, j, k], ag_r.at[q, j, s], dev)
+
+    def ag_got(q, j, s):
+        return rcopy(xa.at[q, j, s], xa.at[q, j, s], ag_s.at[q, j, 0], ag_r.at[q, j, s], sib)
+
+    def at(d):
+        return c * 4 + ring(x + d)
+
+    def ag_copy(q, j, i):
+        d = turn(j)
+        s = (0, 0, 0, -d, -d, d, 2)[i]
+        dev = (xdev(d), xdev(-d), sib, xdev(d), sib, sib, sib)[i]
+        return ag_send(q, j, slot if i < 3 else at(s), i, dev)
+
+    def all_gather(q, sq, gain_row, consume):
+        inv = lax.rsqrt(sq / dim + NORM_EPS)
+        for j in range(NC):
+            gain = gains_v[gain_row:gain_row + 1, j * cw:(j + 1) * cw]
+            xa[q, j, slot] = (hst[j] * inv * gain).astype(jnp.bfloat16).astype(jnp.float32)
+            for k in range(3):
+                ag_copy(q, j, k).start()
+
+        def first(j):
+            d = turn(j)
+            ag_got(q, j, at(-d)).wait_recv()
+            ag_copy(q, j, 3).start()
+            ag_copy(q, j, 4).start()
+            ag_got(q, j, at(d)).wait_recv()
+            ag_copy(q, j, 5).start()
+
+        loop(NC, first)
+
+        def body(j):
+            @pl.when(j < NC)
+            def _():
+                ag_got(q, j, at(2)).wait_recv()
+                ag_copy(q, j, 6).start()
+
+            @pl.when(j >= 1)
+            def _():
+                for k in range(4):
+                    ag_got(q, j - 1, (1 - c) * 4 + k).wait_recv()
+                consume(j - 1, xa[q, j - 1].reshape(2 * half, cw).astype(jnp.bfloat16))
+
+        loop(NC + 1, body)
+
+    def mlp_hidden(q, sq, gain_row, wait_gu):
+        acc[...] = jnp.zeros_like(acc)
+
+        def consume(j, xs):
+            wait_gu(j)
+            acc[:, :mlp] += fdot(xs, wg_v[j])
+            acc[:, mlp:] += fdot(xs, wu_v[j])
+
+        all_gather(q, sq, gain_row, consume)
+        gv = acc[:, :mlp].astype(jnp.bfloat16).astype(jnp.float32)
+        uv = acc[:, mlp:].astype(jnp.bfloat16).astype(jnp.float32)
+        act[...] = (jax.nn.silu(gv) * uv).astype(jnp.bfloat16)
+
+    def part_wo(j):
+        ld_wo(j).wait()
+        return fdot(ob[...], wo_v[j])
+
+    reduce_scatter(0, part_wo)
+    hid_cp.wait()
+    sq = new_rows(0, None)
+
+    def wait_self(j):
+        ld_wg(j).wait()
+        ld_wu(j).wait()
+
+    mlp_hidden(0, sq, 0, wait_self)
+
+    def start_cgu(j):
+        ld_cg(j).start()
+        ld_cu(j).start()
+
+    loop(NC, start_cgu)
+
+    def part_wd(j):
+        ld_wd(j).wait()
+        return fdot(act[...], wd_v[j])
+
+    reduce_scatter(1, part_wd)
+    loop(NC, lambda j: ld_cd(j).start())
+    sq = new_rows(1, None)
+
+    acc[:, :hw] = jnp.zeros((2 * half, hw), jnp.float32)
+
+    def consume_q(j, xs):
+        ld_cq(j).wait()
+        acc[:, :hw] += fdot(xs, cq_v[j])
+
+    all_gather(1, sq, 1, consume_q)
+    qgain = gains_v[3:4, :hd]
+    for h in range(heads):
+        qh = acc[:, h * hd:(h + 1) * hd].astype(jnp.bfloat16).astype(jnp.float32)
+        qinv = lax.rsqrt(jnp.mean(qh * qh, axis=1, keepdims=True) + NORM_EPS)
+        q3[:, h, :] = (qh * qinv * qgain).astype(jnp.bfloat16).astype(jnp.float32)
+    xv_cp.wait()
+
+    def attend(g):
+        ld_kc(g).wait()
+        ld_vc(g).wait()
+        xv = xv_v[pl.ds(pl.multiple_of(g * 8, 8), 8), :]
+        for i in range(8):
+            b = g * 8 + i
+            sc = lax.dot_general(q3[b].astype(jnp.bfloat16), kc_v[b], (((1,), (1,)), ((), ())),
+                                 preferred_element_type=jnp.float32) * scale
+            valid = jnp.broadcast_to(xv[i:i + 1], (8, ntok)) > 0
+            sc = jnp.where(valid, sc, NEG_BIG)
+            mx = jnp.max(sc, axis=1, keepdims=True)
+            pr = jnp.where(valid, jnp.exp(sc - mx), 0.0)
+            ls = jnp.sum(pr, axis=1, keepdims=True)
+            oc[b] = fdot(pr.astype(jnp.bfloat16), vc_v[b]) / ls
+
+    loop(8, attend)
+    for h in range(heads):
+        ob[:, h * hd:(h + 1) * hd] = oc[:, h, :].astype(jnp.bfloat16)
+
+    def part_cwo(j):
+        ld_cwo(j).wait()
+        return fdot(ob[...], cwo_v[j])
+
+    reduce_scatter(2, part_cwo)
+    nrow = rowm_v.shape[1]
+    mine = (y * 8 + slot) * 8 + lax.broadcasted_iota(jnp.int32, (8, nrow), 0)
+    pick = lax.broadcasted_iota(jnp.int32, (8, nrow), 1) == mine
+    rmask = jnp.sum(jnp.where(pick, jnp.broadcast_to(rowm_v[...], (8, nrow)), 0).astype(jnp.float32), axis=1, keepdims=True)
+    factor = [jnp.tanh(jnp.full((8, 128), gate_s[k], jnp.float32))[:, :1] * rmask for k in range(2)]
+    sq = new_rows(2, factor[0])
+
+    def wait_cross(j):
+        ld_cg(j).wait()
+        ld_cu(j).wait()
+
+    mlp_hidden(2, sq, 2, wait_cross)
+
+    def part_cd(j):
+        ld_cd(j).wait()
+        return fdot(act[...], wd_v[j])
+
+    reduce_scatter(3, part_cd)
+    new_rows(3, factor[1])
+
+    def parts_of(j):
+        if j < NC // 2:
+            return (lambda k: og.at[j, c, y, ring(x + k)], xdev), (lambda k: og.at[j, c, ring(y + k)], ydev)
+        return (lambda k: og.at[j, c, ring(y + k), x], ydev), (lambda k: og.at[j, c, :, ring(x + k)], xdev)
+
+    def fg(j, stage, k, s, what, dev):
+        return rcopy(what, what, fg_s.at[j, stage, s], fg_r.at[j, stage, k], dev)
+
+    fg_all = []
+    plans = []
+    for j in range(NC):
+        d = 1 - 2 * (j % 2)
+        stages = []
+        for stage, (region, dev) in enumerate(parts_of(j)):
+            stages.append(dict(
+                own=[fg(j, stage, 0, 0, region(0), dev(d)), fg(j, stage, 1, 1, region(0), dev(-d))],
+                relay=fg(j, stage, 2, 2, region(-d), dev(d)),
+                got=[fg(j, stage, 0, 0, region(-d), sib), fg(j, stage, 1, 1, region(d), sib), fg(j, stage, 2, 2, region(2), sib)],
+                pair=[fg(j, 2, i, i, region(k), sib) for i, k in enumerate((0, -d, d, 2))],
+            ))
+        plans.append(stages)
+    order = []
+    for j in range(NC // 2):
+        order += [j, j + NC // 2]
+    for j in order:
+        og[j, c, y, x] = hst[j]
+        for cp in plans[j][0]['own']:
+            cp.start()
+    for j in order:
+        st = plans[j][0]
+        st['got'][0].wait_recv()
+        st['relay'].start()
+    for j in order:
+        st, nx = plans[j]
+        st['got'][1].wait_recv()
+        st['got'][2].wait_recv()
+        for cp in nx['own']:
+            cp.start()
+        nx['pair'][0].start()
+    for j in order:
+        st = plans[j][1]
+        st['got'][0].wait_recv()
+        st['relay'].start()
+        st['pair'][1].start()
+        st['got'][1].wait_recv()
+        st['pair'][2].start()
+    for j in order:
+        st = plans[j][1]
+        st['got'][2].wait_recv()
+        st['pair'][3].start()
+    for j in order:
+        for cp in plans[j][1]['pair']:
+            cp.wait_recv()
+        for yy in range(4):
+            for cc in range(2):
+                out_v[yy * 8 + cc * 4:yy * 8 + cc * 4 + 4, :, j * cw:(j + 1) * cw] = og[j, cc, yy].astype(jnp.bfloat16)
+
+    for j, d in ((0, 1), (1, -1)):
+        y_relay(j, d).wait_send()
+        y_direct(j, d).wait_send()
+        y_final(j, d).wait_send()
+
+    def drain_rs(j):
+        for p in range(4):
+            rs_pair(p, j).wait_send()
+            rs_relay(p, j).wait_send()
+            rs_direct(p, j).wait_send()
+            rs_final(p, j).wait_send()
+        for q in range(3):
+            for i in range(7):
+                ag_copy(q, j, i).wait_send()
+
+    loop(NC, drain_rs)
+    for j in range(NC):
+        for st in plans[j]:
+            for cp in st['own']:
+                cp.wait_send()
+            st['relay'].wait_send()
+        for cp in plans[j][1]['pair']:
+            cp.wait_send()
+
+
+def tail(blk, hidden, gains, rowmask, gates, xvalid, k_cross, v_cross, wo, wg, wu, wd, cq, cwo, cg, cu, cd, heads, hd):
+    batch, dim = hidden.shape
+    mlp = wg.shape[1]
+    ntok = xvalid.shape[1]
+    cw = dim // NC
+    hw = heads * hd
+    bl = batch // 4
+    half = bl // 2
+    f32, bf16 = jnp.float32, jnp.bfloat16
+    anyspec = pl.BlockSpec(memory_space=pl.ANY)
+    vmem = pl.BlockSpec(memory_space=pltpu.VMEM)
+    smem = pl.BlockSpec(memory_space=pltpu.SMEM)
+    dma = pltpu.SemaphoreType.DMA
+    scratch = [
+        pltpu.VMEM((4, 2, half, hw + hd), f32),
+        pltpu.VMEM((2, half, hw + hd), f32),
+        pltpu.VMEM((2, half, hw + hd), f32),
+        pltpu.VMEM((2, half, hw + hd), f32),
+        pltpu.VMEM((2, half, hw + hd), f32),
+        pltpu.VMEM((bl, hw), bf16),
+        pltpu.VMEM((8, dim), bf16),
+        pltpu.VMEM((NC, 8, cw), f32),
+        pltpu.VMEM((NC, hw, cw), bf16),
+        pltpu.VMEM((NC, cw, mlp), bf16),
+        pltpu.VMEM((NC, cw, mlp), bf16),
+        pltpu.VMEM((NC, mlp, cw), bf16),
+        pltpu.VMEM((NC, cw, hw), bf16),
+        pltpu.VMEM((NC, hw, cw), bf16),
+        pltpu.VMEM((bl, ntok, hd), bf16),
+        pltpu.VMEM((bl, ntok, hd), bf16),
+        pltpu.VMEM((bl, ntok), jnp.int32),
+        pltpu.VMEM((4, NC, 2, half, cw), f32),
+        pltpu.VMEM((4, NC, half, cw), f32),
+        pltpu.VMEM((4, NC, 4, 8, cw), f32),
+        pltpu.VMEM((4, NC, 8, cw), f32),
+        pltpu.VMEM((4, NC, 8, cw), f32),
+        pltpu.VMEM((4, NC, 8, cw), f32),
+        pltpu.VMEM((4, NC, 8, cw), f32),
+        pltpu.VMEM((3, NC, 8, 8, cw), f32),
+        pltpu.VMEM((NC, 2, 4, 4, 8, cw), f32),
+        pltpu.VMEM((bl, 2 * mlp), f32),
+        pltpu.VMEM((bl, mlp), bf16),
+        pltpu.VMEM((bl, 8, hd), f32),
+        pltpu.VMEM((bl, 8, hd), f32),
+        dma((3,)),
+        dma((9, NC)),
+        dma((2, 8)),
+        dma((3, 2)),
+        dma((3, 2)),
+        dma((4, 4, NC)),
+        dma((4, 4, NC)),
+        dma((3, NC, 7)),
+        dma((3, NC, 8)),
+        dma((NC, 3, 4)),
+        dma((NC, 3, 4)),
+    ]
+    out = pl.pallas_call(
+        functools.partial(tail_kernel, (heads, hd, dim, mlp, ntok)),
+        out_shape=jax.ShapeDtypeStruct((batch // 8, 8, dim), bf16),
+        in_specs=[anyspec, anyspec, vmem, vmem, smem] + [anyspec] * 12,
+        out_specs=vmem,
+        scratch_shapes=scratch,
+        compiler_params=pltpu.CompilerParams(collective_id=0, has_side_effects=True, vmem_limit_bytes=67043328),
+        name='tail',
+    )(blk.reshape(4, 2, half, hw + hd), hidden.reshape(batch // 8, 8, dim), gains, rowmask.reshape(1, batch), gates,
+      xvalid.reshape(4, bl, ntok), k_cross.reshape(4, bl, ntok, hd), v_cross.reshape(4, bl, ntok, hd),
+      wo, wg, wu, wd, cq, cwo, cg, cu, cd)
+    return out.reshape(batch, dim)
 
 
 def solution(mesh):
@@ -101,26 +601,15 @@
         k_new_cache = jnp.where(hit_mask, key_new[:, None], k_self)
         v_new_cache = jnp.where(hit_mask, val_new[:, None], v_self)
         seen_mask = (slot_ids[None, :] <= local_pos[:, None])[:, None, None, :]
-        self_stats = local_softmax(queries.reshape(batch_rows, kv_local, group_size, head_dim), k_new_cache, v_new_cache, seen_mask, score_scale)
-        self_attn = combine_sp(self_stats[0], self_stats[1], self_stats[2])
-        self_flat = self_attn.astype(jnp.bfloat16).reshape(batch_rows, heads_local * head_dim)
-        attn_sum = lax.psum(jnp.dot(self_flat, self_wo, preferred_element_type=jnp.float32), 'tp')
-        after_attn = (hidden.astype(jnp.float32) + attn_sum).astype(jnp.bfloat16)
-        mlp_sum = lax.psum(mlp_partial(rms_norm(after_attn, self_mlp_norm), self_wgate, self_wup, self_wdown), 'tp')
-        after_mlp = (after_attn.astype(jnp.float32) + mlp_sum).astype(jnp.bfloat16)
-        normed = rms_norm(after_mlp, cross_attn_norm)
-        cross_q = jnp.dot(normed, cross_wq, preferred_element_type=jnp.float32).astype(jnp.bfloat16)
-        cross_q = rms_norm(cross_q.reshape(batch_rows, heads_local, head_dim), cross_qnorm)
-        cross_mask = (xvalid > 0)[:, None, None, :]
-        cross_stats = local_softmax(cross_q.reshape(batch_rows, kv_local, group_size, head_dim), k_cross, v_cross, cross_mask, score_scale)
-        cross_attn = cross_stats[2] / cross_stats[1][..., None]
-        cross_flat = cross_attn.astype(jnp.bfloat16).reshape(batch_rows, heads_local * head_dim)
-        gate_vals = jnp.tanh(cross_gates.astype(jnp.float32))
-        row_scale = rowmask.astype(jnp.float32)[:, None]
-        xattn_sum = lax.psum(jnp.dot(cross_flat, cross_wo, preferred_element_type=jnp.float32), 'tp')
-        after_cross = (after_mlp.astype(jnp.float32) + gate_vals[0] * row_scale * xattn_sum).astype(jnp.bfloat16)
-        xmlp_sum = lax.psum(mlp_partial(rms_norm(after_cross, cross_mlp_norm), cross_wgate, cross_wup, cross_wdown), 'tp')
-        after_xmlp = (after_cross.astype(jnp.float32) + gate_vals[1] * row_scale * xmlp_sum).astype(jnp.bfloat16)
-        return after_xmlp, k_new_cache, v_new_cache
+        m, l, o = local_softmax(queries.reshape(batch_rows, kv_local, group_size, head_dim), k_new_cache, v_new_cache, seen_mask, score_scale)
+        pad = jnp.zeros((batch_rows, 8 - heads_local), jnp.float32)
+        blk = jnp.concatenate([o.reshape(batch_rows, -1), m.reshape(batch_rows, -1), pad, l.reshape(batch_rows, -1),
+                               jnp.zeros((batch_rows, head_dim - 8 - heads_local), jnp.float32)], axis=1)
+        dim = hidden.shape[1]
+        gains = jnp.stack([self_mlp_norm, cross_attn_norm, cross_mlp_norm,
+                           jnp.pad(cross_qnorm, (0, dim - head_dim))]).astype(jnp.float32)
+        h4 = tail(blk, hidden, gains, rowmask, cross_gates, xvalid, k_cross, v_cross, self_wo, self_wgate, self_wup, self_wdown,
+                  cross_wq, cross_wo, cross_wgate, cross_wup, cross_wdown, heads_local, head_dim)
+        return h4, k_new_cache, v_new_cache
 
     return jax.shard_map(local_step, mesh=mesh, in_specs=in_specs, out_specs=out_specs, check_vma=False)

time: 447 us -> 158 us (0.35)
  waiting for transfers between devices: 280 us -> 0 us
  Pallas kernels: 0 us -> 125 us
  matrix products: 80.3 us -> 9.38 us
  blocking collectives: 29.9 us -> 0 us
  other arithmetic: 31.5 us -> 13.1 us
  between operations: 14.2 us -> 0.84 us
    psum x5 -> x0, waiting for transfers between devices: 279 us -> none  [the longest x1 64.4 us: local_step(): lax.psum(jnp.dot(self_flat, self_wo, preferred_element_type=jnp.float32),...]
    pallas_call x0 -> x1, Pallas kernels: none -> 125 us  [tail(): pl.pallas_call(functools.partial(tail_kernel, (heads, hd, dim, mlp, ntok)...]
    dot_general x7 -> x0, matrix products: 38.1 us -> none  [the longest x2 20.5 us: mlp_partial(): return jnp.dot(hidden_act, w_down, preferred_element_type=jnp.float32)]
    pmax x1 -> x0, blocking collectives: 17.4 us -> none  [combine_sp(): glob_max = lax.pmax(part_max, 'sp')]
    dot_general x2 -> x1, matrix products: 17.1 us -> 1.25 us  [local_softmax(): jnp.einsum('bkgt,btkd->bkgd', probs_loc.astype(jnp.bfloat16), val_rows, p...]
    sub x1 -> x0, matrix products: 14.8 us -> none  [local_softmax(): scores - part_max[..., None]]
    psum x1 -> x0, blocking collectives: 12.6 us -> none  [combine_sp(): total_sum = lax.psum(part_sum * factor, 'sp')]
    reduce_sum x5 -> x1, other arithmetic: 10.1 us -> 1.95 us  [rms_norm(): jnp.mean(vals32 * vals32, axis=-1, keepdims=True) + NORM_EPS]
  transfers between devices with their start and end apart: 5 -> 0, of which waited for: 5 -> 0; matrix products, arithmetic and copies ran while one was open for 0% -> 0% of each run, Pallas kernels for 0% -> 0%
where the time goes in v1:
time: 158 us; the launch traced here: 157 us
  Pallas kernels  125 us (79%)
  other arithmetic  13.1 us (8%)
  local copies, waits for them, and re-layouts  9.42 us (6%)
  matrix products  9.38 us (6%)
    pallas_call x1, Pallas kernels, tail(): pl.pallas_call(functools.partial(tail_kernel, (heads, hd, dim, mlp, ntok)...  125 us
    select_n x1, other arithmetic, local_step(): k_new_cache = jnp.where(hit_mask, key_new[:, None], k_self)  6.97 us
    unnamed x11, local copies, waits for them, and re-layouts  5.13 us

profile of v1, /device:TPU:97, one launch (start us, length us, event | category | flops | bytes accessed | tf_op | source)
XLA Modules:
  0.0 157.3 jit_solution(2263264804807227552)
XLA Ops:
  0.6 0.0 copy-start.1
  0.6 0.0 copy-start.3
  0.7 1.9 %fusion.4 = f32[256]{0:T(256)S(1)} fusion(bf16[256,3072]{1,0:T(8,128)(2,1)} %param.26), kind=kLoop, calls=%fused_computation.8 | loop fusion | flops 2359040 | bytes 1573888 | tf_op jit(solution)/shard_map/reduce_sum | solution.py:43
  2.6 0.8 fusion.41
  3.4 0.7 pad.4
  4.1 0.7 convert_element_type.64
  4.8 0.7 stack.15
  5.5 0.7 stack.16
  6.2 0.7 stack.17
  6.9 0.7 maximum_convert_fusion.gains_v
  7.5 0.1 iota_compare_fusion.1
  7.7 2.3 %convolution_convert_fusion.1 = bf16[256,128]{1,0:T(8,128)(2,1)S(1)} fusion(bf16[3072,128]{1,0:T(8,128)(2,1)} %param.37, bf16[256,3072]{1,0:T(8,128)(2,1)} %param.26, f32[3072]{0:T(1024)S(1)} %convert_element_type.64, f32[256]{0:T(256)S(1)} %add_rsqrt_fusion), kind=kOutput, calls=%fused_computation.15 | convolution fusion | flops 204505088 | bytes 2438144 | tf_op jit(solution)/shard_map/dot_general | solution.py:594
  9.9 0.8 fusion.15
  10.7 0.3 fusion.34
  11.1 0.1 copy.33
  11.2 0.5 multiply_cosine_fusion
  11.7 2.7 %fusion.10 = f32[256,384]{1,0:T(8,128)S(1)} fusion(bf16[3072,384]{1,0:T(8,128)(2,1)} %param.35, bf16[256,3072]{1,0:T(8,128)(2,1)S(1)} %copy-done.1, f32[3072]{0:T(1024)S(1)} %convert_element_type.64, f32[256]{0:T(256)S(1)} %add_rsqrt_fusion), kind=kOutput, calls=%fused_computation.13 | convolution fusion | flops 607322112 | bytes 4338688 | tf_op jit(solution)/shard_map/dot_general | solution.py:592
  14.4 0.2 copy.30
  14.6 0.2 copy.35
  14.9 0.2 copy.34
  15.1 0.3 subtract_convert_fusion
  15.4 7.0 %broadcast_select_fusion.1 = (bf16[256,64,1,128]{3,1,2,0:T(8,128)(2,1)S(1)}, bf16[256,64,1,128]{3,1,2,0:T(8,128)(2,1)S(1)}) fusion(bf16[256,64,1,128]{3,1,2,0:T(8,128)(2,1)} %param.28, pred[256,64]{1,0:T(8,128)(4,1)S(1)} %get-tuple-element.14, bf16[256,128]{1,0:T(8,128)(2,1)S(1)} %copy.33, bf16[256,64,1,128]{3,1,2,0:T(8,128)(2,1)} %param.29, ...), kind=kLoop, calls=%fused_computation.5 | loop fusion | flops 4194304 | bytes 16924672 | tf_op jit(solution)/shard_map/jit(_where)/select_n | solution.py:601
  22.4 0.0 copy-start
  22.4 0.0 copy-start.2
  22.4 2.0 %copy-done = bf16[256,64,1,128]{3,1,2,0:T(8,128)(2,1)} copy-done((bf16[256,64,1,128]{3,1,2,0:T(8,128)(2,1)}, bf16[256,64,1,128]{3,1,2,0:T(8,128)(2,1)S(1)}, u32[]{:S(2)}) %copy-start) | copy-done | bytes 4194328
  24.4 2.4 %fusion.42 = (f32[256,3]{1,0:T(8,128)S(1)}, f32[256,3,64]{2,1,0:T(4,128)S(1)}) fusion(bf16[256,64,1,128]{3,1,2,0:T(8,128)(2,1)S(1)} %get-tuple-element.23, bf16[256,3,64]{2,1,0:T(4,128)(2,1)S(1)} %get-tuple-element.4, bf16[256,3,64]{2,1,0:T(4,128)(2,1)S(1)} %get-tuple-element.3, pred[256,64]{1,0:T(8,128)(4,1)S(1)} %get-tuple-element.13), kind=kOutput, calls=%fused_computation.56 | convolution fusion | flops 13122816 | bytes 4606976 | tf_op jit(solution)/shard_map/bkgd,btkd->bkgt/dot_general | solution.py:48
  26.8 0.7 fusion.16
  27.5 1.2 fusion
  28.8 0.2 concatenate.34
  29.1 1.0 concatenate.37.blk_h
  30.0 124.6 %tail.1 = bf16[32,8,3072]{2,1,0:T(8,128)(2,1)} custom-call(f32[4,2,32,512]{3,2,1,0:T(8,128)} %concatenate.37.blk_h, bf16[32,8,3072]{2,1,0:T(8,128)(2,1)} %bitcast.36, f32[4,3072]{1,0:T(4,128)} %maximum_convert_fusion.gains_v, s32[1,256]{1,0:T(1,128)} %bitcast.41, f32[2]{0:T(128)} %gate_s.1, s32[4,64,512]{2,1,0:T(8,128)} %bitcast.39, ...), custom_call_target="tpu_custom_call" | custom-call | tf_op jit(solution)/shard_map/tail/pallas_call | solution.py:553
  154.7 2.7 %copy.37 = bf16[256,3072]{1,0:T(8,128)(2,1)} copy(bf16[256,3072]{1,0:T(8,128)(2,1)} %bitcast.35) | data formatting | bytes 3145728
  (10 shorter events, 0.1 us)
Async XLA Ops:
  0.6 9.3 %copy-start.1 = (bf16[256,3072]{1,0:T(8,128)(2,1)S(1)}, bf16[256,3072]{1,0:T(8,128)(2,1)}, u32[]{:S(2)}) copy-start(bf16[256,3072]{1,0:T(8,128)(2,1)} %param.26) | copy-start | bytes 4718596
  0.6 9.3 %copy-start.3 = (bf16[3072,128]{1,0:T(8,128)(2,1)S(1)}, bf16[3072,128]{1,0:T(8,128)(2,1)}, u32[]{:S(2)}) copy-start(bf16[3072,128]{1,0:T(8,128)(2,1)} %param.36) | copy-start | bytes 2359300
  22.4 2.0 %copy-start = (bf16[256,64,1,128]{3,1,2,0:T(8,128)(2,1)}, bf16[256,64,1,128]{3,1,2,0:T(8,128)(2,1)S(1)}, u32[]{:S(2)}) copy-start(bf16[256,64,1,128]{3,1,2,0:T(8,128)(2,1)S(1)} %get-tuple-element.23) | copy-start | bytes 12582916
  22.4 5.2 %copy-start.2 = (bf16[256,64,1,128]{3,1,2,0:T(8,128)(2,1)}, bf16[256,64,1,128]{3,1,2,0:T(8,128)(2,1)S(1)}, u32[]{:S(2)}) copy-start(bf16[256,64,1,128]{3,1,2,0:T(8,128)(2,1)S(1)} %get-tuple-element.24) | copy-start | bytes 12582916

commit v2 on v1

--- a/solution.py
+++ b/solution.py
@@ -2,6 +2,7 @@
 import math
 import jax
 import jax.numpy as jnp
+import numpy as np
 from jax import lax
 from jax.experimental import pallas as pl
 from jax.experimental.pallas import tpu as pltpu
@@ -19,46 +20,181 @@
 
 
 def rope_freqs(head_dim):
-    inv_freq = 1.0 / (ROPE_THETA ** (jnp.arange(0, head_dim, 2).astype(jnp.float32) / head_dim))
+    inv_freq = (1.0 / (ROPE_THETA ** (np.arange(0, head_dim, 2).astype(np.float32) / np.float32(head_dim)))).astype(np.float32)
     wavelen = 2.0 * math.pi / inv_freq
     smooth = (ORIG_CTX / wavelen - LOW_FREQ) / (HIGH_FREQ - LOW_FREQ)
     mid_freq = (1.0 - smooth) * inv_freq / ROPE_FACTOR + smooth * inv_freq
-    scaled = jnp.where(wavelen > ORIG_CTX / LOW_FREQ, inv_freq / ROPE_FACTOR, mid_freq)
-    return jnp.where(wavelen < ORIG_CTX / HIGH_FREQ, inv_freq, scaled)
-
-
-def apply_rope(vectors, positions):
-    head_dim = vectors.shape[-1]
-    half_dim = head_dim // 2
-    angles = positions.astype(jnp.float32)[:, None] * rope_freqs(head_dim)[None, :]
-    cos_t = jnp.cos(angles)[:, None, :]
-    sin_t = jnp.sin(angles)[:, None, :]
-    first_half = vectors[..., :half_dim]
-    second_half = vectors[..., half_dim:]
-    return jnp.concatenate([first_half * cos_t - second_half * sin_t, second_half * cos_t + first_half * sin_t], axis=-1)
-
-
-def rms_norm(values, gain_vec):
-    vals32 = values.astype(jnp.float32)
-    inv_rms = lax.rsqrt(jnp.mean(vals32 * vals32, axis=-1, keepdims=True) + NORM_EPS)
-    return (vals32 * inv_rms * gain_vec.astype(jnp.float32)).astype(jnp.bfloat16)
-
-
-def local_softmax(queries, key_rows, val_rows, valid_mask, score_scale):
-    scores = jnp.einsum('bkgd,btkd->bkgt', queries, key_rows, preferred_element_type=jnp.float32) * score_scale
-    scores = jnp.where(valid_mask, scores, NEG_BIG)
-    part_max = jnp.max(scores, axis=-1)
-    probs_loc = jnp.where(valid_mask, jnp.exp(scores - part_max[..., None]), 0.0)
-    part_sum = jnp.sum(probs_loc, axis=-1)
-    part_out = jnp.einsum('bkgt,btkd->bkgd', probs_loc.astype(jnp.bfloat16), val_rows, preferred_element_type=jnp.float32)
-    return part_max, part_sum, part_out
+    scaled = np.where(wavelen > ORIG_CTX / LOW_FREQ, inv_freq / ROPE_FACTOR, mid_freq)
+    half = np.where(wavelen < ORIG_CTX / HIGH_FREQ, inv_freq, scaled).astype(np.float32)
+    return np.concatenate([half, half])[None, :]
 
 
 def fdot(a, b):
     return jnp.dot(a, b, preferred_element_type=jnp.float32)
 
 
-def tail_kernel(cfg, blk_h, hid_h, gains_v, rowm_v, gate_s, xv_h, kc_h, vc_h,
+def front_kernel(cfg, hid_h, posr_v, pos_s, gain_v, freq_v, wq_h, wk_h, wv_h, k_h, v_h, ko_h, vo_h, blk_v,
+                 hid_v, xn, wq_v, wk_v, wv_v, kc, vc, q3, o3, st3, kn, vn, in_sem, kv_sem, out_sem):
+    heads, hd, dim, batch, slots = cfg
+    f32, bf16 = jnp.float32, jnp.bfloat16
+    per = 32
+    nch = batch // per
+    scale = hd ** -0.5
+    first_slot = lax.axis_index('sp') * slots
+
+    def loop(n, body):
+        def step(i, carry):
+            body(i)
+            return carry
+        lax.fori_loop(0, n, step, 0)
+
+    def ld_hid(r):
+        span = pl.ds(pl.multiple_of(r * per, per), per)
+        return pltpu.make_async_copy(hid_h.at[span], hid_v.at[span], in_sem.at[3 + r])
+
+    weights = [pltpu.make_async_copy(h, v, in_sem.at[i]) for i, (h, v) in enumerate(((wq_h, wq_v), (wk_h, wk_v), (wv_h, wv_v)))]
+
+    def ld_kv(g):
+        span = pl.ds(g * per, per)
+        return (pltpu.make_async_copy(k_h.at[span], kc.at[span], kv_sem.at[0, g]),
+                pltpu.make_async_copy(v_h.at[span], vc.at[span], kv_sem.at[1, g]))
+
+    def st_kv(g):
+        span = pl.ds(g * per, per)
+        return (pltpu.make_async_copy(kc.at[span], ko_h.at[span], out_sem.at[0, g]),
+                pltpu.make_async_copy(vc.at[span], vo_h.at[span], out_sem.at[1, g]))
+
+    def start_both(pair):
+        pair[0].start()
+        pair[1].start()
+
+    def wait_both(pair):
+        pair[0].wait()
+        pair[1].wait()
+
+    loop(nch, lambda r: ld_hid(r).start())
+    for cp in weights:
+        cp.start()
+    loop(nch, lambda g: start_both(ld_kv(g)))
+    q3[...] = jnp.zeros_like(q3)
+
+    gain = gain_v[...].astype(f32)
+
+    def norm(r):
+        ld_hid(r).wait()
+        span = pl.ds(pl.multiple_of(r * per, per), per)
+        xs = hid_v[span, :].astype(f32)
+        inv = lax.rsqrt(jnp.sum(xs * xs, axis=1, keepdims=True) / dim + NORM_EPS)
+        for k in range(dim // 128):
+            xn[span, k * 128:(k + 1) * 128] = (xs[:, k * 128:(k + 1) * 128] * inv * gain[k:k + 1]).astype(bf16)
+
+    loop(nch, norm)
+    eye = lax.broadcasted_iota(jnp.int32, (batch, batch), 0) == lax.broadcasted_iota(jnp.int32, (batch, batch), 1)
+    posc = jnp.sum(jnp.where(eye, jnp.broadcast_to(posr_v[...], (batch, batch)).astype(f32), 0.0), axis=1, keepdims=True)
+    angles = posc * freq_v[...]
+    cos_t = jnp.cos(angles)
+    low = lax.broadcasted_iota(jnp.int32, (batch, hd), 1) < hd // 2
+    sin_t = jnp.where(low, -jnp.sin(angles), jnp.sin(angles))
+
+    def rope(v):
+        r = v.astype(bf16).astype(f32)
+        return (r * cos_t + pltpu.roll(r, hd // 2, 1) * sin_t).astype(bf16).astype(f32)
+
+    for cp in weights:
+        cp.wait()
+    q = fdot(xn[...], wq_v[...])
+    for h in range(heads):
+        q3[:, h, :] = rope(q[:, h * hd:(h + 1) * hd])
+    kn[...] = rope(fdot(xn[...], wk_v[...]))
+    vn[...] = fdot(xn[...], wv_v[...]).astype(bf16).astype(f32)
+
+    lane = lax.broadcasted_iota(jnp.int32, (8, 128), 1)
+    sub = lax.broadcasted_iota(jnp.int32, (8, 128), 0)
+    row16 = lax.broadcasted_iota(jnp.int32, (16, hd), 0)
+    zero = jnp.zeros((8, 128), f32)
+
+    def attend(g):
+        wait_both(ld_kv(g))
+        lps = []
+        for i in range(per):
+            b = g * per + i
+            lp = pos_s[b] - first_slot
+            lps.append(lp)
+            base = pl.multiple_of(lax.shift_left(lax.shift_right_logical(jnp.clip(lp, 0, slots - 1), 4), 4), 16)
+            hit = row16 + base == lp
+            for ref, new in ((kc, kn), (vc, vn)):
+                old = ref[b, pl.ds(base, 16), :].astype(f32)
+                fresh = jnp.broadcast_to(new[pl.ds(b, 1), :], (16, hd))
+                ref[b, pl.ds(base, 16), :] = jnp.where(hit, fresh, old).astype(bf16)
+        start_both(st_kv(g))
+        for t in range(per // 4):
+            four = pl.ds(g * per + 4 * t, 4)
+            sg = lax.dot_general(q3[four].reshape(32, hd).astype(bf16), kc[four].reshape(4 * slots, hd),
+                                 (((1,), (1,)), ((), ())), preferred_element_type=f32) * scale
+            probs = []
+            for i in range(4):
+                off = slots * (i % 2)
+                lp = jnp.minimum(lps[4 * t + i], slots - 1)
+                seen = (lane >= off) & (lane <= off + lp)
+                sc = jnp.where(seen, sg[8 * i:8 * i + 8, 128 * (i // 2):128 * (i // 2) + 128], NEG_BIG)
+                mx = jnp.max(sc, axis=1, keepdims=True)
+                pr = jnp.where(seen, jnp.exp(sc - mx), 0.0)
+                ls = jnp.sum(pr, axis=1, keepdims=True)
+                st3[g * per + 4 * t + i] = jnp.where(lane == sub, mx, jnp.where(lane == sub + 8, ls, 0.0))
+                probs.append(jnp.concatenate([pr, zero] if i < 2 else [zero, pr], axis=1))
+            pg = jnp.concatenate(probs, axis=0).astype(bf16)
+            o3[four] = fdot(pg, vc[four].reshape(4 * slots, hd)).reshape(4, 8, hd)
+
+    loop(nch, attend)
+    stat = st3[:, 0, :]
+    for h in range(1, heads):
+        stat = stat + st3[:, h, :]
+    for h in range(heads):
+        blk_v[:, h * hd:(h + 1) * hd] = o3[:, h, :]
+    blk_v[:, heads * hd:] = stat
+    loop(nch, lambda g: wait_both(st_kv(g)))
+
+
+def front(hidden, new_pos, k_self, v_self, gain, wq, wk, wv, heads, hd):
+    batch, dim = hidden.shape
+    slots = k_self.shape[1]
+    f32, bf16 = jnp.float32, jnp.bfloat16
+    anyspec = pl.BlockSpec(memory_space=pl.ANY)
+    vmem = pl.BlockSpec(memory_space=pltpu.VMEM)
+    smem = pl.BlockSpec(memory_space=pltpu.SMEM)
+    dma = pltpu.SemaphoreType.DMA
+    nch = batch // 32
+    cache = jax.ShapeDtypeStruct((batch, slots, hd), bf16)
+    ko, vo, blk = pl.pallas_call(
+        functools.partial(front_kernel, (heads, hd, dim, batch, slots)),
+        out_shape=(cache, cache, jax.ShapeDtypeStruct((batch, heads * hd + hd), f32)),
+        in_specs=[anyspec, vmem, smem, vmem, vmem] + [anyspec] * 5,
+        out_specs=(anyspec, anyspec, vmem),
+        scratch_shapes=[
+            pltpu.VMEM((batch, dim), bf16),
+            pltpu.VMEM((batch, dim), bf16),
+            pltpu.VMEM(wq.shape, bf16),
+            pltpu.VMEM(wk.shape, bf16),
+            pltpu.VMEM(wv.shape, bf16),
+            pltpu.VMEM((batch, slots, hd), bf16),
+            pltpu.VMEM((batch, slots, hd), bf16),
+            pltpu.VMEM((batch, 8, hd), f32),
+            pltpu.VMEM((batch, 8, hd), f32),
+            pltpu.VMEM((batch, 8, hd), f32),
+            pltpu.VMEM((batch, hd), f32),
+            pltpu.VMEM((batch, hd), f32),
+            dma((3 + nch,)),
+            dma((2, nch)),
+            dma((2, nch)),
+        ],
+        compiler_params=pltpu.CompilerParams(vmem_limit_bytes=60000000),
+        name='front',
+    )(hidden, new_pos.reshape(1, batch), new_pos, gain.reshape(dim // 128, 128), jnp.asarray(rope_freqs(hd)),
+      wq, wk, wv, k_self.reshape(batch, slots, hd), v_self.reshape(batch, slots, hd))
+    return ko.reshape(k_self.shape), vo.reshape(v_self.shape), blk
+
+
+def tail_kernel(cfg, blk_h, hid_h, g2_v, g3_v, g4_v, qn_v, rowm_v, gate_s, xv_h, kc_h, vc_h,
                 wo_h, wg_h, wu_h, wd_h, cq_h, cwo_h, cg_h, cu_h, cd_h, out_v,
                 bk, yr, yd, yt, yf, ob, hrow, hst,
                 wo_v, wg_v, wu_v, wd_v, cq_v, cwo_v, kc_v, vc_v, xv_v,
@@ -283,8 +419,9 @@
 
     def all_gather(q, sq, gain_row, consume):
         inv = lax.rsqrt(sq / dim + NORM_EPS)
+        rows_of = (g2_v, g3_v, g4_v)[gain_row][...].astype(jnp.float32)
         for j in range(NC):
-            gain = gains_v[gain_row:gain_row + 1, j * cw:(j + 1) * cw]
+            gain = jnp.concatenate([rows_of[i:i + 1] for i in range(j * cw // 128, (j + 1) * cw // 128)], axis=1)
             xa[q, j, slot] = (hst[j] * inv * gain).astype(jnp.bfloat16).astype(jnp.float32)
             for k in range(3):
                 ag_copy(q, j, k).start()
@@ -361,7 +498,7 @@
         acc[:, :hw] += fdot(xs, cq_v[j])
 
     all_gather(1, sq, 1, consume_q)
-    qgain = gains_v[3:4, :hd]
+    qgain = qn_v[...].astype(jnp.float32)
     for h in range(heads):
         qh = acc[:, h * hd:(h + 1) * hd].astype(jnp.bfloat16).astype(jnp.float32)
         qinv = lax.rsqrt(jnp.mean(qh * qh, axis=1, keepdims=True) + NORM_EPS)
@@ -553,12 +690,13 @@
     out = pl.pallas_call(
         functools.partial(tail_kernel, (heads, hd, dim, mlp, ntok)),
         out_shape=jax.ShapeDtypeStruct((batch // 8, 8, dim), bf16),
-        in_specs=[anyspec, anyspec, vmem, vmem, smem] + [anyspec] * 12,
+        in_specs=[anyspec, anyspec] + [vmem] * 5 + [smem] + [anyspec] * 12,
         out_specs=vmem,
         scratch_shapes=scratch,
         compiler_params=pltpu.CompilerParams(collective_id=0, has_side_effects=True, vmem_limit_bytes=67043328),
         name='tail',
-    )(blk.reshape(4, 2, half, hw + hd), hidden.reshape(batch // 8, 8, dim), gains, rowmask.reshape(1, batch), gates,
+    )(blk.reshape(4, 2, half, hw + hd), hidden.reshape(batch // 8, 8, dim),
+      *[g.reshape(-1, 128) for g in gains], rowmask.reshape(1, batch), gates,
       xvalid.reshape(4, bl, ntok), k_cross.reshape(4, bl, ntok, hd), v_cross.reshape(4, bl, ntok, hd),
       wo, wg, wu, wd, cq, cwo, cg, cu, cd)
     return out.reshape(batch, dim)
@@ -581,33 +719,11 @@
                    self_attn_norm, self_wq, self_wk, self_wv, self_wo, self_mlp_norm,
                    self_wgate, self_wup, self_wdown, cross_attn_norm, cross_wq, cross_qnorm,
                    cross_wo, cross_gates, cross_mlp_norm, cross_wgate, cross_wup, cross_wdown):
-        batch_rows = hidden.shape[0]
-        len_local = k_self.shape[1]
-        kv_local = k_self.shape[2]
         head_dim = k_self.shape[3]
         heads_local = self_wq.shape[1] // head_dim
-        group_size = heads_local // kv_local
-        score_scale = head_dim ** -0.5
-        normed = rms_norm(hidden, self_attn_norm)
-        queries = jnp.dot(normed, self_wq, preferred_element_type=jnp.float32).astype(jnp.bfloat16)
-        key_new = jnp.dot(normed, self_wk, preferred_element_type=jnp.float32).astype(jnp.bfloat16)
-        val_new = jnp.dot(normed, self_wv, preferred_element_type=jnp.float32).astype(jnp.bfloat16)
-        queries = apply_rope(queries.reshape(batch_rows, heads_local, head_dim).astype(jnp.float32), new_pos).astype(jnp.bfloat16)
-        key_new = apply_rope(key_new.reshape(batch_rows, kv_local, head_dim).astype(jnp.float32), new_pos).astype(jnp.bfloat16)
-        val_new = val_new.reshape(batch_rows, kv_local, head_dim)
-        local_pos = new_pos - lax.axis_index('sp') * len_local
-        slot_ids = jnp.arange(len_local)
-        hit_mask = (slot_ids[None, :] == local_pos[:, None])[:, :, None, None]
-        k_new_cache = jnp.where(hit_mask, key_new[:, None], k_self)
-        v_new_cache = jnp.where(hit_mask, val_new[:, None], v_self)
-        seen_mask = (slot_ids[None, :] <= local_pos[:, None])[:, None, None, :]
-        m, l, o = local_softmax(queries.reshape(batch_rows, kv_local, group_size, head_dim), k_new_cache, v_new_cache, seen_mask, score_scale)
-        pad = jnp.zeros((batch_rows, 8 - heads_local), jnp.float32)
-        blk = jnp.concatenate([o.reshape(batch_rows, -1), m.reshape(batch_rows, -1), pad, l.reshape(batch_rows, -1),
-                               jnp.zeros((batch_rows, head_dim - 8 - heads_local), jnp.float32)], axis=1)
-        dim = hidden.shape[1]
-        gains = jnp.stack([self_mlp_norm, cross_attn_norm, cross_mlp_norm,
-                           jnp.pad(cross_qnorm, (0, dim - head_dim))]).astype(jnp.float32)
+        k_new_cache, v_new_cache, blk = front(hidden, new_pos, k_self, v_self, self_attn_norm, self_wq, self_wk, self_wv,
+                                              heads_local, head_dim)
+        gains = (self_mlp_norm, cross_attn_norm, cross_mlp_norm, cross_qnorm)
         h4 = tail(blk, hidden, gains, rowmask, cross_gates, xvalid, k_cross, v_cross, self_wo, self_wgate, self_wup, self_wdown,
                   cross_wq, cross_wo, cross_wgate, cross_wup, cross_wdown, heads_local, head_dim)
         return h4, k_new_cache, v_new_cache

time: 158 us -> 153 us (0.968)
  Pallas kernels: 125 us -> 150 us
  other arithmetic: 13.1 us -> 0 us
  matrix products: 9.38 us -> 0 us
  local copies, waits for them, and re-layouts: 9.42 us -> 2.65 us
    pallas_call x0 -> x1, Pallas kernels: none -> 25 us  [front(): pl.pallas_call(functools.partial(front_kernel, (heads, hd, dim, batch, sl...]
    dot_general x5 -> x0, matrix products: 9.38 us -> none  [the longest x1 2.69 us: local_step(): jnp.dot(normed, self_wq, preferred_element_type=jnp.float32)]
    select_n x2 -> x0, other arithmetic: 6.98 us -> none  [the longest x1 6.97 us: local_step(): k_new_cache = jnp.where(hit_mask, key_new[:, None], k_self)]
    reduce_sum x2 -> x0, other arithmetic: 2.69 us -> none  [the longest x1 1.95 us: rms_norm(): jnp.mean(vals32 * vals32, axis=-1, keepdims=True) + NORM_EPS]
    unnamed x11 -> x1, local copies, waits for them, and re-layouts: 5.13 us -> 2.65 us
    convert_element_type x3 -> x0, other arithmetic: 2.14 us -> none  [the longest x1 0.76 us: apply_rope(): positions.astype(jnp.float32)[:, None] * rope_freqs(head_dim)[None, :]]
    another operation x4 -> x0, local copies, waits for them, and re-layouts: 2.11 us -> none  [local_step(): jnp.stack([self_mlp_norm, cross_attn_norm, cross_mlp_norm, jnp.pad(cross_...]
where the time goes in v2:
time: 153 us
  Pallas kernels  150 us (98%)
  local copies, waits for them, and re-layouts  2.65 us (2%)
    pallas_call x1, Pallas kernels, tail(): pl.pallas_call(functools.partial(tail_kernel, (heads, hd, dim, mlp, ntok)...  125 us
    pallas_call x1, Pallas kernels, front(): pl.pallas_call(functools.partial(front_kernel, (heads, hd, dim, batch, sl...  25 us

profile of v2, /device:TPU:97, one launch (start us, length us, event | category | flops | bytes accessed | tf_op | source)
XLA Modules:
  0.0 152.9 jit_solution(17367178846499710049)
XLA Ops:
  0.6 25.0 %front.1 = (bf16[256,64,128]{2,1,0:T(8,128)(2,1)}, bf16[256,64,128]{2,1,0:T(8,128)(2,1)}, f32[256,512]{1,0:T(8,128)}) custom-call(bf16[256,3072]{1,0:T(8,128)(2,1)} %hid_h.1, s32[1,256]{1,0:T(1,128)} %bitcast.33, s32[256]{0:T(256)} %pos_s.1, bf16[24,128]{1,0:T(8,128)(2,1)} %bitcast.29, f32[1,128]{1,0:T(1,128)} %constant.2.clone.freq_v, ...), custom_call_target="tpu_custom_call" | custom-call | tf_op jit(solution)/shard_map/front/pallas_call | solution.py:168
  25.7 124.6 %tail.1 = bf16[32,8,3072]{2,1,0:T(8,128)(2,1)} custom-call(f32[4,2,32,512]{3,2,1,0:T(8,128)} %bitcast.28, bf16[32,8,3072]{2,1,0:T(8,128)(2,1)} %bitcast.23, bf16[24,128]{1,0:T(8,128)(2,1)} %bitcast.30, bf16[24,128]{1,0:T(8,128)(2,1)} %bitcast.31, bf16[24,128]{1,0:T(8,128)(2,1)} %bitcast.32, bf16[1,128]{1,0:T(2,128)(2,1)} %bitcast.35, s32[1,256]{1,0:T(1,128)} %bitcast.34, ...), custom_call_target="tpu_custom_call" | custom-call | tf_op jit(solution)/shard_map/tail/pallas_call | solution.py:690
  150.3 2.7 %copy.33 = bf16[256,3072]{1,0:T(8,128)(2,1)} copy(bf16[256,3072]{1,0:T(8,128)(2,1)} %bitcast.24) | data formatting | bytes 3145728

commit v3 on v2

--- a/solution.py
+++ b/solution.py
@@ -127,23 +127,43 @@
                 fresh = jnp.broadcast_to(new[pl.ds(b, 1), :], (16, hd))
                 ref[b, pl.ds(base, 16), :] = jnp.where(hit, fresh, old).astype(bf16)
         start_both(st_kv(g))
-        for t in range(per // 4):
-            four = pl.ds(g * per + 4 * t, 4)
-            sg = lax.dot_general(q3[four].reshape(32, hd).astype(bf16), kc[four].reshape(4 * slots, hd),
-                                 (((1,), (1,)), ((), ())), preferred_element_type=f32) * scale
-            probs = []
+        fours = [pl.ds(g * per + 4 * t, 4) for t in range(per // 4)]
+
+        def scores(ts):
+            return [lax.dot_general(q3[fours[t]].reshape(32, hd).astype(bf16), kc[fours[t]].reshape(4 * slots, hd),
+                                    (((1,), (1,)), ((), ())), preferred_element_type=f32) * scale for t in ts]
+
+        def soften(ts, sgs):
+            out = []
+            for t, sg in zip(ts, sgs):
+                probs, stats = [], []
+                for i in range(4):
+                    off = slots * (i % 2)
+                    lp = jnp.minimum(lps[4 * t + i], slots - 1)
+                    seen = (lane >= off) & (lane <= off + lp)
+                    sc = jnp.where(seen, sg[8 * i:8 * i + 8, 128 * (i // 2):128 * (i // 2) + 128], NEG_BIG)
+                    mx = jnp.max(sc, axis=1, keepdims=True)
+                    pr = jnp.where(seen, jnp.exp(sc - mx), 0.0)
+                    ls = jnp.sum(pr, axis=1, keepdims=True)
+                    stats.append(jnp.where(lane == sub, mx, jnp.where(lane == sub + 8, ls, 0.0)))
+                    probs.append(jnp.concatenate([pr, zero] if i < 2 else [zero, pr], axis=1))
+                out.append((jnp.concatenate(probs, axis=0).astype(bf16), stats))
+            return out
+
+        def mix(ts, prs):
+            return [fdot(pg, vc[fours[t]].reshape(4 * slots, hd)) for t, (pg, _) in zip(ts, prs)]
+
+        one, two = range(per // 8), range(per // 8, per // 4)
+        sa = scores(one)
+        sb = scores(two)
+        pa = soften(one, sa)
+        oa = mix(one, pa)
+        pb = soften(two, sb)
+        o2 = mix(two, pb)
+        for t, (o, (_, stats)) in enumerate(zip(oa + o2, pa + pb)):
+            o3[fours[t]] = o.reshape(4, 8, hd)
             for i in range(4):
-                off = slots * (i % 2)
-                lp = jnp.minimum(lps[4 * t + i], slots - 1)
-                seen = (lane >= off) & (lane <= off + lp)
-                sc = jnp.where(seen, sg[8 * i:8 * i + 8, 128 * (i // 2):128 * (i // 2) + 128], NEG_BIG)
-                mx = jnp.max(sc, axis=1, keepdims=True)
-                pr = jnp.where(seen, jnp.exp(sc - mx), 0.0)
-                ls = jnp.sum(pr, axis=1, keepdims=True)
-                st3[g * per + 4 * t + i] = jnp.where(lane == sub, mx, jnp.where(lane == sub + 8, ls, 0.0))
-                probs.append(jnp.concatenate([pr, zero] if i < 2 else [zero, pr], axis=1))
-            pg = jnp.concatenate(probs, axis=0).astype(bf16)
-            o3[four] = fdot(pg, vc[four].reshape(4 * slots, hd)).reshape(4, 8, hd)
+                st3[g * per + 4 * t + i] = stats[i]
 
     loop(nch, attend)
     stat = st3[:, 0, :]
@@ -505,22 +525,40 @@
         q3[:, h, :] = (qh * qinv * qgain).astype(jnp.bfloat16).astype(jnp.float32)
     xv_cp.wait()
 
-    def attend(g):
-        ld_kc(g).wait()
-        ld_vc(g).wait()
-        xv = xv_v[pl.ds(pl.multiple_of(g * 8, 8), 8), :]
-        for i in range(8):
-            b = g * 8 + i
-            sc = lax.dot_general(q3[b].astype(jnp.bfloat16), kc_v[b], (((1,), (1,)), ((), ())),
-                                 preferred_element_type=jnp.float32) * scale
-            valid = jnp.broadcast_to(xv[i:i + 1], (8, ntok)) > 0
-            sc = jnp.where(valid, sc, NEG_BIG)
-            mx = jnp.max(sc, axis=1, keepdims=True)
-            pr = jnp.where(valid, jnp.exp(sc - mx), 0.0)
-            ls = jnp.sum(pr, axis=1, keepdims=True)
-            oc[b] = fdot(pr.astype(jnp.bfloat16), vc_v[b]) / ls
-
-    loop(8, attend)
+    nat = 16
+
+    def attend(t):
+        for u in range(nat // 8):
+            ld_kc(t * (nat // 8) + u).wait()
+            ld_vc(t * (nat // 8) + u).wait()
+
+        def scores(us):
+            return [lax.dot_general(q3[t * nat + u].astype(jnp.bfloat16), kc_v[t * nat + u], (((1,), (1,)), ((), ())),
+                                    preferred_element_type=jnp.float32) * scale for u in us]
+
+        def soften(us, scs):
+            out = []
+            for u, sc in zip(us, scs):
+                valid = jnp.broadcast_to(xvs[u // 8][u % 8:u % 8 + 1], (8, ntok)) > 0
+                sc = jnp.where(valid, sc, NEG_BIG)
+                mx = jnp.max(sc, axis=1, keepdims=True)
+                pr = jnp.where(valid, jnp.exp(sc - mx), 0.0)
+                out.append((pr.astype(jnp.bfloat16), jnp.sum(pr, axis=1, keepdims=True)))
+            return out
+
+        def mix(us, prs):
+            return [fdot(pr, vc_v[t * nat + u]) / ls for u, (pr, ls) in zip(us, prs)]
+
+        xvs = [xv_v[pl.ds(pl.multiple_of(t * nat + 8 * u, 8), 8), :] for u in range(nat // 8)]
+        one, two = range(nat // 2), range(nat // 2, nat)
+        sa = scores(one)
+        sb = scores(two)
+        oa = mix(one, soften(one, sa))
+        o2 = mix(two, soften(two, sb))
+        for u, o in enumerate(oa + o2):
+            oc[t * nat + u] = o
+
+    loop(2 * half // nat, attend)
     for h in range(heads):
         ob[:, h * hd:(h + 1) * hd] = oc[:, h, :].astype(jnp.bfloat16)
 
@@ -547,7 +585,6 @@
         return fdot(act[...], wd_v[j])
 
     reduce_scatter(3, part_cd)
-    new_rows(3, factor[1])
 
     def parts_of(j):
         if j < NC // 2:
@@ -570,11 +607,9 @@
                 pair=[fg(j, 2, i, i, region(k), sib) for i, k in enumerate((0, -d, d, 2))],
             ))
         plans.append(stages)
-    order = []
-    for j in range(NC // 2):
-        order += [j, j + NC // 2]
+    order = range(NC)
     for j in order:
-        og[j, c, y, x] = hst[j]
+        og[j, c, y, x] = (hst[j] + factor[1] * reduced(3, j)).astype(jnp.bfloat16).astype(jnp.float32)
         for cp in plans[j][0]['own']:
             cp.start()
     for j in order:

time: 153 us -> 127 us (0.83)
  Pallas kernels: 150 us -> 124 us
    pallas_call x1, Pallas kernels: 125 us -> 111 us  [tail(): pl.pallas_call(functools.partial(tail_kernel, (heads, hd, dim, mlp, ntok)...]
    pallas_call x1, Pallas kernels: 25 us -> 13.3 us  [front(): pl.pallas_call(functools.partial(front_kernel, (heads, hd, dim, batch, sl...]
where the time goes in v3:
time: 127 us
  Pallas kernels  124 us (98%)
  local copies, waits for them, and re-layouts  2.65 us (2%)
    pallas_call x1, Pallas kernels, tail(): pl.pallas_call(functools.partial(tail_kernel, (heads, hd, dim, mlp, ntok)...  111 us
    pallas_call x1, Pallas kernels, front(): pl.pallas_call(functools.partial(front_kernel, (heads, hd, dim, batch, sl...  13.3 us
    unnamed x1, local copies, waits for them, and re-layouts  2.65 us

profile of v3, /device:TPU:97, one launch (start us, length us, event | category | flops | bytes accessed | tf_op | source)
XLA Modules:
  0.0 127.2 jit_solution(9946257764248973417)
XLA Ops:
  0.6 13.3 %front.1 = (bf16[256,64,128]{2,1,0:T(8,128)(2,1)}, bf16[256,64,128]{2,1,0:T(8,128)(2,1)}, f32[256,512]{1,0:T(8,128)}) custom-call(bf16[256,3072]{1,0:T(8,128)(2,1)} %hid_h.1, s32[1,256]{1,0:T(1,128)} %bitcast.33, s32[256]{0:T(256)} %pos_s.1, bf16[24,128]{1,0:T(8,128)(2,1)} %bitcast.29, f32[1,128]{1,0:T(1,128)} %constant.2.clone.freq_v, ...), custom_call_target="tpu_custom_call" | custom-call | tf_op jit(solution)/shard_map/front/pallas_call | solution.py:188
  14.0 110.5 %tail.1 = bf16[32,8,3072]{2,1,0:T(8,128)(2,1)} custom-call(f32[4,2,32,512]{3,2,1,0:T(8,128)} %bitcast.28, bf16[32,8,3072]{2,1,0:T(8,128)(2,1)} %bitcast.23, bf16[24,128]{1,0:T(8,128)(2,1)} %bitcast.30, bf16[24,128]{1,0:T(8,128)(2,1)} %bitcast.31, bf16[24,128]{1,0:T(8,128)(2,1)} %bitcast.32, bf16[1,128]{1,0:T(2,128)(2,1)} %bitcast.35, s32[1,256]{1,0:T(1,128)} %bitcast.34, ...), custom_call_target="tpu_custom_call" | custom-call | tf_op jit(solution)/shard_map/tail/pallas_call | solution.py:725
  124.5 2.7 %copy.33 = bf16[256,3072]{1,0:T(8,128)(2,1)} copy(bf16[256,3072]{1,0:T(8,128)(2,1)} %bitcast.24) | data formatting | bytes 3145728

commit v4 on v3

--- a/solution.py
+++ b/solution.py
@@ -218,8 +218,8 @@
                 wo_h, wg_h, wu_h, wd_h, cq_h, cwo_h, cg_h, cu_h, cd_h, out_v,
                 bk, yr, yd, yt, yf, ob, hrow, hst,
                 wo_v, wg_v, wu_v, wd_v, cq_v, cwo_v, kc_v, vc_v, xv_v,
-                pbuf, dbuf, sbuf, rbuf, ebuf, tbuf, fbuf, xa, og, acc, act, q3, oc,
-                ld_sem, w_sem, kv_sem, ys, yrs, rs_s, rs_r, ag_s, ag_r, fg_s, fg_r):
+                pbuf, dbuf, s0, s1, r1, r2, xa, og, acc, act, q3, oc, fac,
+                ld_sem, w_sem, kv_sem, ys, yrs, pr_s, pr_r, ar_s, ar_r, lr_s, lr_r, xs_s, xs_r, fg_s, fg_r):
     heads, hd, dim, mlp, ntok = cfg
     cw = dim // NC
     hw = heads * hd
@@ -227,7 +227,8 @@
     x = lax.axis_index('tp') // 2
     c = lax.axis_index('tp') % 2
     y = lax.axis_index('sp')
-    slot = c * 4 + x
+    flip = x + 1 - 2 * lax.rem(x, 2)
+    cross = 3 - x
     scale = hd ** -0.5
 
     def ring(v):
@@ -252,7 +253,7 @@
         lax.fori_loop(0, n, step, 0)
 
     blk_cp = pltpu.make_async_copy(blk_h, bk, ld_sem.at[0])
-    hid_cp = pltpu.make_async_copy(hid_h.at[y * 8 + slot], hrow, ld_sem.at[1])
+    hid_cp = pltpu.make_async_copy(hid_h.at[y * 2 + c], hrow, ld_sem.at[1])
     xv_cp = pltpu.make_async_copy(xv_h.at[y], xv_v, ld_sem.at[2])
 
     def cols(h, v, k, j):
@@ -318,6 +319,12 @@
     loop(8, start_kv)
     loop(NC, lambda j: ld_cwo(j).start())
     q3[...] = jnp.zeros_like(q3)
+    nrow = rowm_v.shape[1]
+    mine = (y * 2 + c) * half + lax.broadcasted_iota(jnp.int32, (half, nrow), 0)
+    pick = lax.broadcasted_iota(jnp.int32, (half, nrow), 1) == mine
+    rmask = jnp.sum(jnp.where(pick, jnp.broadcast_to(rowm_v[...], (half, nrow)), 0).astype(jnp.float32), axis=1, keepdims=True)
+    for k in range(2):
+        fac[k] = (jnp.tanh(jnp.full((half, 128), gate_s[k], jnp.float32)) * rmask).reshape(4, 8, 128)
     pl.semaphore_wait(barrier, 5)
 
     lane = lax.broadcasted_iota(jnp.int32, (half, hd), 1)
@@ -364,111 +371,113 @@
         for h in range(heads):
             ob[j * half:(j + 1) * half, h * hd:(h + 1) * hd] = (both[:, h * hd:(h + 1) * hd] / sums[h]).astype(jnp.bfloat16)
 
-    def rs_pair(p, j):
-        return rcopy(pbuf.at[p, j, 1 - c], dbuf.at[p, j], rs_s.at[p, 0, j], rs_r.at[p, 0, j], sib)
-
-    def turn(j):
-        return 1 - 2 * lax.rem(j, 2)
-
-    def rs_relay(p, j):
-        return rcopy(sbuf.at[p, j, ring(x + 2)], rbuf.at[p, j], rs_s.at[p, 1, j], rs_r.at[p, 1, j], xdev(turn(j)))
-
-    def rs_direct(p, j):
-        return rcopy(sbuf.at[p, j, ring(x - turn(j))], ebuf.at[p, j], rs_s.at[p, 2, j], rs_r.at[p, 2, j], xdev(-turn(j)))
-
-    def rs_final(p, j):
-        return rcopy(tbuf.at[p, j], fbuf.at[p, j], rs_s.at[p, 3, j], rs_r.at[p, 3, j], xdev(turn(j)))
-
-    def reduce_scatter(p, partial):
-        def second(j):
-            rs_pair(p, j).wait_recv()
-            sbuf[p, j] = (pbuf[p, j, c] + dbuf[p, j]).reshape(4, 8, cw)
-            rs_relay(p, j).start()
-            rs_direct(p, j).start()
-
+    def pair_cp(j):
+        return rcopy(pbuf.at[j, 1 - c], dbuf.at[j], pr_s.at[j], pr_r.at[j], sib)
+
+    def mate(j, second):
+        odd = lax.rem(j + second, 2)
+        return {'tp': 2 * (flip + odd * (cross - flip)) + c}
+
+    def one_cp(p, j):
+        return rcopy(s0.at[j], r1.at[p % 2, j], ar_s.at[0, j], ar_r.at[p % 2, 0, j], mate(j, 0))
+
+    def two_cp(p, j):
+        return rcopy(s1.at[j], r2.at[p % 2, j], ar_s.at[1, j], ar_r.at[p % 2, 1, j], mate(j, 1))
+
+    def pair_sums(p, partial, after):
         def body(j):
             @pl.when(j < NC)
             def _():
-                pbuf[p, j] = partial(j).reshape(2, half, cw)
-                rs_pair(p, j).start()
+                if p > 0:
+                    pair_cp(j).wait_send()
+                pbuf[j] = partial(j).reshape(2, half, cw)
+                pair_cp(j).start()
 
             @pl.when(j >= 1)
             def _():
-                second(j - 1)
+                pair_cp(j - 1).wait_recv()
+                if p > 0:
+                    one_cp(p, j - 1).wait_send()
+                s0[j - 1] = (pbuf[j - 1, c] + dbuf[j - 1]).reshape(4, 8, cw)
+                after(j - 1)
 
         loop(NC + 1, body)
 
-        def third(j):
-            rs_relay(p, j).wait_recv()
-            tbuf[p, j] = sbuf[p, j, ring(x + turn(j))] + rbuf[p, j]
-            rs_final(p, j).start()
-
-        loop(NC, third)
-
-    def reduced(p, j):
-        rs_direct(p, j).wait_recv()
-        rs_final(p, j).wait_recv()
-        return sbuf[p, j, x] + ebuf[p, j] + fbuf[p, j]
-
-    def new_rows(p, factor):
-        sq = jnp.zeros((8, 1), jnp.float32)
+    def all_reduce(p, partial):
+        pair_sums(p, partial, lambda j: one_cp(p, j).start())
+
+        def step(j):
+            one_cp(p, j).wait_recv()
+            if p > 0:
+                two_cp(p, j).wait_send()
+            s1[j] = s0[j] + r1[p % 2, j]
+            two_cp(p, j).start()
+
+        loop(NC, step)
+
+    def new_rows(p, k):
+        sq = jnp.zeros((4, 8, 1), jnp.float32)
         for j in range(NC):
-            add = reduced(p, j)
-            if factor is not None:
-                add = factor * add
-            old = hrow[:, j * cw:(j + 1) * cw].astype(jnp.float32) if p == 0 else hst[j]
+            two_cp(p, j).wait_recv()
+            add = s1[j] + r2[p % 2, j]
+            if k is not None:
+                add = fac[k][:, :, :1] * add
+            old = hrow[:, :, j * cw:(j + 1) * cw].astype(jnp.float32) if p == 0 else hst[j]
             new = (old + add).astype(jnp.bfloat16).astype(jnp.float32)
             hst[j] = new
-            sq = sq + jnp.sum(new * new, axis=1, keepdims=True)
+            sq = sq + jnp.sum(new * new, axis=2, keepdims=True)
         return sq
 
-    def ag_send(q, j, s, k, dev):
-        return rcopy(xa.at[q, j, s], xa.at[q, j, s], ag_s.at[q, j, k], ag_r.at[q, j, s], dev)
-
-    def ag_got(q, j, s):
-        return rcopy(xa.at[q, j, s], xa.at[q, j, s], ag_s.at[q, j, 0], ag_r.at[q, j, s], sib)
-
-    def at(d):
-        return c * 4 + ring(x + d)
-
-    def ag_copy(q, j, i):
-        d = turn(j)
-        s = (0, 0, 0, -d, -d, d, 2)[i]
-        dev = (xdev(d), xdev(-d), sib, xdev(d), sib, sib, sib)[i]
-        return ag_send(q, j, slot if i < 3 else at(s), i, dev)
+    def swap_cp(j):
+        return rcopy(xa.at[j, c], xa.at[j, c], xs_s.at[j], xs_r.at[j], sib)
 
     def all_gather(q, sq, gain_row, consume):
         inv = lax.rsqrt(sq / dim + NORM_EPS)
         rows_of = (g2_v, g3_v, g4_v)[gain_row][...].astype(jnp.float32)
         for j in range(NC):
             gain = jnp.concatenate([rows_of[i:i + 1] for i in range(j * cw // 128, (j + 1) * cw // 128)], axis=1)
-            xa[q, j, slot] = (hst[j] * inv * gain).astype(jnp.bfloat16).astype(jnp.float32)
-            for k in range(3):
-                ag_copy(q, j, k).start()
-
-        def first(j):
-            d = turn(j)
-            ag_got(q, j, at(-d)).wait_recv()
-            ag_copy(q, j, 3).start()
-            ag_copy(q, j, 4).start()
-            ag_got(q, j, at(d)).wait_recv()
-            ag_copy(q, j, 5).start()
-
-        loop(NC, first)
+            if q > 0:
+                swap_cp(j).wait_send()
+            xa[j, c] = (hst[j] * inv * gain.reshape(1, 1, cw)).astype(jnp.bfloat16).astype(jnp.float32).reshape(half, cw)
+            swap_cp(j).start()
 
         def body(j):
-            @pl.when(j < NC)
-            def _():
-                ag_got(q, j, at(2)).wait_recv()
-                ag_copy(q, j, 6).start()
-
-            @pl.when(j >= 1)
-            def _():
-                for k in range(4):
-                    ag_got(q, j - 1, (1 - c) * 4 + k).wait_recv()
-                consume(j - 1, xa[q, j - 1].reshape(2 * half, cw).astype(jnp.bfloat16))
-
-        loop(NC + 1, body)
+            swap_cp(j).wait_recv()
+            consume(j, xa[j].reshape(2 * half, cw).astype(jnp.bfloat16))
+
+        loop(NC, body)
+
+    def turn(j):
+        return 1 - 2 * lax.rem(j, 2)
+
+    def relay_cp(j):
+        return rcopy(s0.at[j, ring(x + 2)], r1.at[1, j, 0], lr_s.at[0, j], lr_r.at[0, j], xdev(turn(j)))
+
+    def direct_cp(j):
+        return rcopy(s0.at[j, ring(x - turn(j))], r1.at[1, j, 1], lr_s.at[1, j], lr_r.at[1, j], xdev(-turn(j)))
+
+    def last_cp(j):
+        return rcopy(s1.at[j, 0], r1.at[1, j, 2], lr_s.at[2, j], lr_r.at[2, j], xdev(turn(j)))
+
+    def last_scatter(partial):
+        def send(j):
+            relay_cp(j).start()
+            direct_cp(j).start()
+
+        pair_sums(3, partial, send)
+
+        def step(j):
+            relay_cp(j).wait_recv()
+            two_cp(2, j).wait_send()
+            s1[j, 0] = s0[j, ring(x + turn(j))] + r1[1, j, 0]
+            last_cp(j).start()
+
+        loop(NC, step)
+
+    def last_rows(j):
+        direct_cp(j).wait_recv()
+        last_cp(j).wait_recv()
+        return s0[j, x] + r1[1, j, 1] + r1[1, j, 2]
 
     def mlp_hidden(q, sq, gain_row, wait_gu):
         acc[...] = jnp.zeros_like(acc)
@@ -487,7 +496,7 @@
         ld_wo(j).wait()
         return fdot(ob[...], wo_v[j])
 
-    reduce_scatter(0, part_wo)
+    all_reduce(0, part_wo)
     hid_cp.wait()
     sq = new_rows(0, None)
 
@@ -507,7 +516,7 @@
         ld_wd(j).wait()
         return fdot(act[...], wd_v[j])
 
-    reduce_scatter(1, part_wd)
+    all_reduce(1, part_wd)
     loop(NC, lambda j: ld_cd(j).start())
     sq = new_rows(1, None)
 
@@ -566,13 +575,8 @@
         ld_cwo(j).wait()
         return fdot(ob[...], cwo_v[j])
 
-    reduce_scatter(2, part_cwo)
-    nrow = rowm_v.shape[1]
-    mine = (y * 8 + slot) * 8 + lax.broadcasted_iota(jnp.int32, (8, nrow), 0)
-    pick = lax.broadcasted_iota(jnp.int32, (8, nrow), 1) == mine
-    rmask = jnp.sum(jnp.where(pick, jnp.broadcast_to(rowm_v[...], (8, nrow)), 0).astype(jnp.float32), axis=1, keepdims=True)
-    factor = [jnp.tanh(jnp.full((8, 128), gate_s[k], jnp.float32))[:, :1] * rmask for k in range(2)]
-    sq = new_rows(2, factor[0])
+    all_reduce(2, part_cwo)
+    sq = new_rows(2, 0)
 
     def wait_cross(j):
         ld_cg(j).wait()
@@ -584,7 +588,7 @@
         ld_cd(j).wait()
         return fdot(act[...], wd_v[j])
 
-    reduce_scatter(3, part_cd)
+    last_scatter(part_cd)
 
     def parts_of(j):
         if j < NC // 2:
@@ -609,7 +613,7 @@
         plans.append(stages)
     order = range(NC)
     for j in order:
-        og[j, c, y, x] = (hst[j] + factor[1] * reduced(3, j)).astype(jnp.bfloat16).astype(jnp.float32)
+        og[j, c, y, x] = (hst[j, x] + fac[1, x][:, :1] * last_rows(j)).astype(jnp.bfloat16).astype(jnp.float32)
         for cp in plans[j][0]['own']:
             cp.start()
     for j in order:
@@ -646,17 +650,14 @@
         y_direct(j, d).wait_send()
         y_final(j, d).wait_send()
 
-    def drain_rs(j):
-        for p in range(4):
-            rs_pair(p, j).wait_send()
-            rs_relay(p, j).wait_send()
-            rs_direct(p, j).wait_send()
-            rs_final(p, j).wait_send()
-        for q in range(3):
-            for i in range(7):
-                ag_copy(q, j, i).wait_send()
-
-    loop(NC, drain_rs)
+    def drain(j):
+        pair_cp(j).wait_send()
+        swap_cp(j).wait_send()
+        relay_cp(j).wait_send()
+        direct_cp(j).wait_send()
+        last_cp(j).wait_send()
+
+    loop(NC, drain)
     for j in range(NC):
         for st in plans[j]:
             for cp in st['own']:
@@ -686,8 +687,8 @@
         pltpu.VMEM((2, half, hw + hd), f32),
         pltpu.VMEM((2, half, hw + hd), f32),
         pltpu.VMEM((bl, hw), bf16),
-        pltpu.VMEM((8, dim), bf16),
-        pltpu.VMEM((NC, 8, cw), f32),
+        pltpu.VMEM((4, 8, dim), bf16),
+        pltpu.VMEM((NC, 4, 8, cw), f32),
         pltpu.VMEM((NC, hw, cw), bf16),
         pltpu.VMEM((NC, cw, mlp), bf16),
         pltpu.VMEM((NC, cw, mlp), bf16),
@@ -697,28 +698,32 @@
         pltpu.VMEM((bl, ntok, hd), bf16),
         pltpu.VMEM((bl, ntok, hd), bf16),
         pltpu.VMEM((bl, ntok), jnp.int32),
-        pltpu.VMEM((4, NC, 2, half, cw), f32),
-        pltpu.VMEM((4, NC, half, cw), f32),
-        pltpu.VMEM((4, NC, 4, 8, cw), f32),
-        pltpu.VMEM((4, NC, 8, cw), f32),
-        pltpu.VMEM((4, NC, 8, cw), f32),
-        pltpu.VMEM((4, NC, 8, cw), f32),
-        pltpu.VMEM((4, NC, 8, cw), f32),
-        pltpu.VMEM((3, NC, 8, 8, cw), f32),
+        pltpu.VMEM((NC, 2, half, cw), f32),
+        pltpu.VMEM((NC, half, cw), f32),
+        pltpu.VMEM((NC, 4, 8, cw), f32),
+        pltpu.VMEM((NC, 4, 8, cw), f32),
+        pltpu.VMEM((2, NC, 4, 8, cw), f32),
+        pltpu.VMEM((2, NC, 4, 8, cw), f32),
+        pltpu.VMEM((NC, 2, half, cw), f32),
         pltpu.VMEM((NC, 2, 4, 4, 8, cw), f32),
         pltpu.VMEM((bl, 2 * mlp), f32),
         pltpu.VMEM((bl, mlp), bf16),
         pltpu.VMEM((bl, 8, hd), f32),
         pltpu.VMEM((bl, 8, hd), f32),
+        pltpu.VMEM((2, 4, 8, 128), f32),
         dma((3,)),
         dma((9, NC)),
         dma((2, 8)),
         dma((3, 2)),
         dma((3, 2)),
-        dma((4, 4, NC)),
-        dma((4, 4, NC)),
-        dma((3, NC, 7)),
-        dma((3, NC, 8)),
+        dma((NC,)),
+        dma((NC,)),
+        dma((2, NC)),
+        dma((2, 2, NC)),
+        dma((3, NC)),
+        dma((3, NC)),
+        dma((NC,)),
+        dma((NC,)),
         dma((NC, 3, 4)),
         dma((NC, 3, 4)),
     ]
@@ -730,7 +735,7 @@
         scratch_shapes=scratch,
         compiler_params=pltpu.CompilerParams(collective_id=0, has_side_effects=True, vmem_limit_bytes=67043328),
         name='tail',
-    )(blk.reshape(4, 2, half, hw + hd), hidden.reshape(batch // 8, 8, dim),
+    )(blk.reshape(4, 2, half, hw + hd), hidden.reshape(8, 4, 8, dim),
       *[g.reshape(-1, 128) for g in gains], rowmask.reshape(1, batch), gates,
       xvalid.reshape(4, bl, ntok), k_cross.reshape(4, bl, ntok, hd), v_cross.reshape(4, bl, ntok, hd),
       wo, wg, wu, wd, cq, cwo, cg, cu, cd)

time: 127 us -> 114 us (0.90)
  Pallas kernels: 124 us -> 111 us
    pallas_call x1, Pallas kernels: 111 us -> 97.6 us  [tail(): pl.pallas_call(functools.partial(tail_kernel, (heads, hd, dim, mlp, ntok)...]
where the time goes in v4:
time: 114 us
  Pallas kernels  111 us (97%)
  local copies, waits for them, and re-layouts  2.65 us (2%)
    pallas_call x1, Pallas kernels, tail(): pl.pallas_call(functools.partial(tail_kernel, (heads, hd, dim, mlp, ntok)...  97.6 us
    pallas_call x1, Pallas kernels, front(): pl.pallas_call(functools.partial(front_kernel, (heads, hd, dim, batch, sl...  13.3 us
    unnamed x1, local copies, waits for them, and re-layouts  2.65 us

profile of v4, /device:TPU:97, one launch (start us, length us, event | category | flops | bytes accessed | tf_op | source)
XLA Modules:
  0.0 114.2 jit_solution(5631859964755007886)
XLA Ops:
  0.6 13.3 %front.1 = (bf16[256,64,128]{2,1,0:T(8,128)(2,1)}, bf16[256,64,128]{2,1,0:T(8,128)(2,1)}, f32[256,512]{1,0:T(8,128)}) custom-call(bf16[256,3072]{1,0:T(8,128)(2,1)} %hid_h.1, s32[1,256]{1,0:T(1,128)} %bitcast.33, s32[256]{0:T(256)} %pos_s.1, bf16[24,128]{1,0:T(8,128)(2,1)} %bitcast.29, f32[1,128]{1,0:T(1,128)} %constant.2.clone.freq_v, ...), custom_call_target="tpu_custom_call" | custom-call | tf_op jit(solution)/shard_map/front/pallas_call | solution.py:188
  14.0 97.6 %tail.1 = bf16[32,8,3072]{2,1,0:T(8,128)(2,1)} custom-call(f32[4,2,32,512]{3,2,1,0:T(8,128)} %bitcast.28, bf16[8,4,8,3072]{3,2,1,0:T(8,128)(2,1)} %bitcast.23, bf16[24,128]{1,0:T(8,128)(2,1)} %bitcast.30, bf16[24,128]{1,0:T(8,128)(2,1)} %bitcast.31, bf16[24,128]{1,0:T(8,128)(2,1)} %bitcast.32, bf16[1,128]{1,0:T(2,128)(2,1)} %bitcast.35, s32[1,256]{1,0:T(1,128)} %bitcast.34, ...), custom_call_target="tpu_custom_call" | custom-call | tf_op jit(solution)/shard_map/tail/pallas_call | solution.py:730
  111.5 2.7 %copy.33 = bf16[256,3072]{1,0:T(8,128)(2,1)} copy(bf16[256,3072]{1,0:T(8,128)(2,1)} %bitcast.24) | data formatting | bytes 3145728

commit v5 on v4

--- a/solution.py
+++ b/solution.py
@@ -15,7 +15,7 @@
 HIGH_FREQ = 4.0
 ORIG_CTX = 8192.0
 NEG_BIG = -1e30
-NC = 4
+NC = 6
 MESH = pl.DeviceIdType.MESH
 
 
@@ -34,11 +34,12 @@
 
 
 def front_kernel(cfg, hid_h, posr_v, pos_s, gain_v, freq_v, wq_h, wk_h, wv_h, k_h, v_h, ko_h, vo_h, blk_v,
-                 hid_v, xn, wq_v, wk_v, wv_v, kc, vc, q3, o3, st3, kn, vn, in_sem, kv_sem, out_sem):
+                 hid_v, xn, wq_v, wkv_v, kc, vc, q3, o3, st3, kn, vn, in_sem, kv_sem, out_sem):
     heads, hd, dim, batch, slots = cfg
     f32, bf16 = jnp.float32, jnp.bfloat16
-    per = 32
+    per = 64
     nch = batch // per
+    nrm = 32
     scale = hd ** -0.5
     first_slot = lax.axis_index('sp') * slots
 
@@ -49,10 +50,11 @@
         lax.fori_loop(0, n, step, 0)
 
     def ld_hid(r):
-        span = pl.ds(pl.multiple_of(r * per, per), per)
+        span = pl.ds(pl.multiple_of(r * nrm, nrm), nrm)
         return pltpu.make_async_copy(hid_h.at[span], hid_v.at[span], in_sem.at[3 + r])
 
-    weights = [pltpu.make_async_copy(h, v, in_sem.at[i]) for i, (h, v) in enumerate(((wq_h, wq_v), (wk_h, wk_v), (wv_h, wv_v)))]
+    weights = [pltpu.make_async_copy(h, v, in_sem.at[i])
+               for i, (h, v) in enumerate(((wq_h, wq_v), (wk_h, wkv_v.at[:, :hd]), (wv_h, wkv_v.at[:, hd:])))]
 
     def ld_kv(g):
         span = pl.ds(g * per, per)
@@ -72,7 +74,7 @@
         pair[0].wait()
         pair[1].wait()
 
-    loop(nch, lambda r: ld_hid(r).start())
+    loop(batch // nrm, lambda r: ld_hid(r).start())
     for cp in weights:
         cp.start()
     loop(nch, lambda g: start_both(ld_kv(g)))
@@ -82,13 +84,13 @@
 
     def norm(r):
         ld_hid(r).wait()
-        span = pl.ds(pl.multiple_of(r * per, per), per)
+        span = pl.ds(pl.multiple_of(r * nrm, nrm), nrm)
         xs = hid_v[span, :].astype(f32)
         inv = lax.rsqrt(jnp.sum(xs * xs, axis=1, keepdims=True) / dim + NORM_EPS)
         for k in range(dim // 128):
             xn[span, k * 128:(k + 1) * 128] = (xs[:, k * 128:(k + 1) * 128] * inv * gain[k:k + 1]).astype(bf16)
 
-    loop(nch, norm)
+    loop(batch // nrm, norm)
     eye = lax.broadcasted_iota(jnp.int32, (batch, batch), 0) == lax.broadcasted_iota(jnp.int32, (batch, batch), 1)
     posc = jnp.sum(jnp.where(eye, jnp.broadcast_to(posr_v[...], (batch, batch)).astype(f32), 0.0), axis=1, keepdims=True)
     angles = posc * freq_v[...]
@@ -105,8 +107,9 @@
     q = fdot(xn[...], wq_v[...])
     for h in range(heads):
         q3[:, h, :] = rope(q[:, h * hd:(h + 1) * hd])
-    kn[...] = rope(fdot(xn[...], wk_v[...]))
-    vn[...] = fdot(xn[...], wv_v[...]).astype(bf16).astype(f32)
+    kv = fdot(xn[...], wkv_v[...])
+    kn[...] = rope(kv[:, :hd])
+    vn[...] = kv[:, hd:].astype(bf16).astype(f32)
 
     lane = lax.broadcasted_iota(jnp.int32, (8, 128), 1)
     sub = lax.broadcasted_iota(jnp.int32, (8, 128), 0)
@@ -153,14 +156,15 @@
         def mix(ts, prs):
             return [fdot(pg, vc[fours[t]].reshape(4 * slots, hd)) for t, (pg, _) in zip(ts, prs)]
 
-        one, two = range(per // 8), range(per // 8, per // 4)
-        sa = scores(one)
-        sb = scores(two)
-        pa = soften(one, sa)
-        oa = mix(one, pa)
-        pb = soften(two, sb)
-        o2 = mix(two, pb)
-        for t, (o, (_, stats)) in enumerate(zip(oa + o2, pa + pb)):
+        sets = [range(t, t + 4) for t in range(0, per // 4, 4)]
+        raw, soft, mixed = [scores(sets[0])], [], []
+        for k, ts in enumerate(sets):
+            if k + 1 < len(sets):
+                raw.append(scores(sets[k + 1]))
+            soft.append(soften(ts, raw[k]))
+            mixed += mix(ts, soft[k])
+        flat = [st for sf in soft for _, st in sf]
+        for t, (o, stats) in enumerate(zip(mixed, flat)):
             o3[fours[t]] = o.reshape(4, 8, hd)
             for i in range(4):
                 st3[g * per + 4 * t + i] = stats[i]
@@ -183,7 +187,7 @@
     vmem = pl.BlockSpec(memory_space=pltpu.VMEM)
     smem = pl.BlockSpec(memory_space=pltpu.SMEM)
     dma = pltpu.SemaphoreType.DMA
-    nch = batch // 32
+    nch = batch // 64
     cache = jax.ShapeDtypeStruct((batch, slots, hd), bf16)
     ko, vo, blk = pl.pallas_call(
         functools.partial(front_kernel, (heads, hd, dim, batch, slots)),
@@ -194,8 +198,7 @@
             pltpu.VMEM((batch, dim), bf16),
             pltpu.VMEM((batch, dim), bf16),
             pltpu.VMEM(wq.shape, bf16),
-            pltpu.VMEM(wk.shape, bf16),
-            pltpu.VMEM(wv.shape, bf16),
+            pltpu.VMEM((dim, 2 * hd), bf16),
             pltpu.VMEM((batch, slots, hd), bf16),
             pltpu.VMEM((batch, slots, hd), bf16),
             pltpu.VMEM((batch, 8, hd), f32),
@@ -203,7 +206,7 @@
             pltpu.VMEM((batch, 8, hd), f32),
             pltpu.VMEM((batch, hd), f32),
             pltpu.VMEM((batch, hd), f32),
-            dma((3 + nch,)),
+            dma((3 + batch // 32,)),
             dma((2, nch)),
             dma((2, nch)),
         ],
@@ -215,11 +218,11 @@
 
 
 def tail_kernel(cfg, blk_h, hid_h, g2_v, g3_v, g4_v, qn_v, rowm_v, gate_s, xv_h, kc_h, vc_h,
-                wo_h, wg_h, wu_h, wd_h, cq_h, cwo_h, cg_h, cu_h, cd_h, out_v,
+                wo_h, wg_h, wu_h, wd_h, cq_h, cwo_h, cg_h, cu_h, cd_h, out_h,
                 bk, yr, yd, yt, yf, ob, hrow, hst,
                 wo_v, wg_v, wu_v, wd_v, cq_v, cwo_v, kc_v, vc_v, xv_v,
                 pbuf, dbuf, s0, s1, r1, r2, xa, og, acc, act, q3, oc, fac,
-                ld_sem, w_sem, kv_sem, ys, yrs, pr_s, pr_r, ar_s, ar_r, lr_s, lr_r, xs_s, xs_r, fg_s, fg_r):
+                ld_sem, w_sem, kv_sem, ys, yrs, pr_s, pr_r, ar_s, ar_r, lr_s, lr_r, xs_s, xs_r, fg_s, fg_r, out_sem):
     heads, hd, dim, mlp, ntok = cfg
     cw = dim // NC
     hw = heads * hd
@@ -301,7 +304,7 @@
     loop(NC, lambda j: ld_wo(j).start())
 
     barrier = pltpu.get_barrier_semaphore()
-    for dev in (sib, xdev(1), xdev(-1), ydev(1), ydev(-1)):
+    for dev in (sib, xdev(1), xdev(2), xdev(-1), ydev(1), ydev(2), ydev(-1)):
         pl.semaphore_signal(barrier, inc=1, device_id=dev, device_id_type=MESH)
 
     def start_gu(j):
@@ -325,7 +328,7 @@
     rmask = jnp.sum(jnp.where(pick, jnp.broadcast_to(rowm_v[...], (half, nrow)), 0).astype(jnp.float32), axis=1, keepdims=True)
     for k in range(2):
         fac[k] = (jnp.tanh(jnp.full((half, 128), gate_s[k], jnp.float32)) * rmask).reshape(4, 8, 128)
-    pl.semaphore_wait(barrier, 5)
+    pl.semaphore_wait(barrier, 7)
 
     lane = lax.broadcasted_iota(jnp.int32, (half, hd), 1)
 
@@ -441,11 +444,13 @@
             xa[j, c] = (hst[j] * inv * gain.reshape(1, 1, cw)).astype(jnp.bfloat16).astype(jnp.float32).reshape(half, cw)
             swap_cp(j).start()
 
-        def body(j):
-            swap_cp(j).wait_recv()
-            consume(j, xa[j].reshape(2 * half, cw).astype(jnp.bfloat16))
-
-        loop(NC, body)
+        def body(t):
+            swap_cp(2 * t).wait_recv()
+            swap_cp(2 * t + 1).wait_recv()
+            xs = [xa[2 * t + u].reshape(2 * half, cw).astype(jnp.bfloat16) for u in range(2)]
+            consume(t, jnp.concatenate(xs, axis=1))
+
+        loop(NC // 2, body)
 
     def turn(j):
         return 1 - 2 * lax.rem(j, 2)
@@ -482,10 +487,12 @@
     def mlp_hidden(q, sq, gain_row, wait_gu):
         acc[...] = jnp.zeros_like(acc)
 
-        def consume(j, xs):
-            wait_gu(j)
-            acc[:, :mlp] += fdot(xs, wg_v[j])
-            acc[:, mlp:] += fdot(xs, wu_v[j])
+        def consume(t, xs):
+            wait_gu(2 * t)
+            wait_gu(2 * t + 1)
+            two = pl.ds(2 * t, 2)
+            acc[:, :mlp] += fdot(xs, wg_v[two].reshape(2 * cw, mlp))
+            acc[:, mlp:] += fdot(xs, wu_v[two].reshape(2 * cw, mlp))
 
         all_gather(q, sq, gain_row, consume)
         gv = acc[:, :mlp].astype(jnp.bfloat16).astype(jnp.float32)
@@ -522,9 +529,10 @@
 
     acc[:, :hw] = jnp.zeros((2 * half, hw), jnp.float32)
 
-    def consume_q(j, xs):
-        ld_cq(j).wait()
-        acc[:, :hw] += fdot(xs, cq_v[j])
+    def consume_q(t, xs):
+        ld_cq(2 * t).wait()
+        ld_cq(2 * t + 1).wait()
+        acc[:, :hw] += fdot(xs, cq_v[pl.ds(2 * t, 2)].reshape(2 * cw, hw))
 
     all_gather(1, sq, 1, consume_q)
     qgain = qn_v[...].astype(jnp.float32)
@@ -598,17 +606,19 @@
     def fg(j, stage, k, s, what, dev):
         return rcopy(what, what, fg_s.at[j, stage, s], fg_r.at[j, stage, k], dev)
 
-    fg_all = []
     plans = []
     for j in range(NC):
         d = 1 - 2 * (j % 2)
         stages = []
         for stage, (region, dev) in enumerate(parts_of(j)):
+            own = [fg(j, stage, 0, 0, region(0), dev(d)), fg(j, stage, 1, 1, region(0), dev(-d))]
+            if stage == 0:
+                own.append(fg(j, stage, 2, 2, region(0), dev(2)))
             stages.append(dict(
-                own=[fg(j, stage, 0, 0, region(0), dev(d)), fg(j, stage, 1, 1, region(0), dev(-d))],
-                relay=fg(j, stage, 2, 2, region(-d), dev(d)),
+                own=own,
+                relay=[fg(j, stage, 2, 2, region(-d), dev(d))] if stage else [],
                 got=[fg(j, stage, 0, 0, region(-d), sib), fg(j, stage, 1, 1, region(d), sib), fg(j, stage, 2, 2, region(2), sib)],
-                pair=[fg(j, 2, i, i, region(k), sib) for i, k in enumerate((0, -d, d, 2))],
+                pair=[fg(j, 2, i, i, region(k), sib) for i, k in enumerate((0, -d, d, 2))] if stage else [],
             ))
         plans.append(stages)
     order = range(NC)
@@ -617,33 +627,32 @@
         for cp in plans[j][0]['own']:
             cp.start()
     for j in order:
-        st = plans[j][0]
-        st['got'][0].wait_recv()
-        st['relay'].start()
-    for j in order:
         st, nx = plans[j]
-        st['got'][1].wait_recv()
-        st['got'][2].wait_recv()
+        for cp in st['got']:
+            cp.wait_recv()
         for cp in nx['own']:
             cp.start()
         nx['pair'][0].start()
     for j in order:
         st = plans[j][1]
         st['got'][0].wait_recv()
-        st['relay'].start()
+        st['relay'][0].start()
         st['pair'][1].start()
         st['got'][1].wait_recv()
         st['pair'][2].start()
+
+    def result_cp(j, cc):
+        return pltpu.make_async_copy(og.at[j, cc], out_h.at[:, cc, :, :, j * cw:(j + 1) * cw], out_sem.at[cc, j])
+
     for j in order:
         st = plans[j][1]
         st['got'][2].wait_recv()
         st['pair'][3].start()
+        result_cp(j, c).start()
     for j in order:
         for cp in plans[j][1]['pair']:
             cp.wait_recv()
-        for yy in range(4):
-            for cc in range(2):
-                out_v[yy * 8 + cc * 4:yy * 8 + cc * 4 + 4, :, j * cw:(j + 1) * cw] = og[j, cc, yy].astype(jnp.bfloat16)
+        result_cp(j, 1 - c).start()
 
     for j, d in ((0, 1), (1, -1)):
         y_relay(j, d).wait_send()
@@ -660,11 +669,11 @@
     loop(NC, drain)
     for j in range(NC):
         for st in plans[j]:
-            for cp in st['own']:
+            for cp in st['own'] + st['relay'] + st['pair']:
                 cp.wait_send()
-            st['relay'].wait_send()
-        for cp in plans[j][1]['pair']:
-            cp.wait_send()
+    for j in order:
+        result_cp(j, 0).wait()
+        result_cp(j, 1).wait()
 
 
 def tail(blk, hidden, gains, rowmask, gates, xvalid, k_cross, v_cross, wo, wg, wu, wd, cq, cwo, cg, cu, cd, heads, hd):
@@ -726,12 +735,13 @@
         dma((NC,)),
         dma((NC, 3, 4)),
         dma((NC, 3, 4)),
+        dma((2, NC)),
     ]
     out = pl.pallas_call(
         functools.partial(tail_kernel, (heads, hd, dim, mlp, ntok)),
-        out_shape=jax.ShapeDtypeStruct((batch // 8, 8, dim), bf16),
+        out_shape=jax.ShapeDtypeStruct((4, 2, 4, 8, dim), f32),
         in_specs=[anyspec, anyspec] + [vmem] * 5 + [smem] + [anyspec] * 12,
-        out_specs=vmem,
+        out_specs=anyspec,
         scratch_shapes=scratch,
         compiler_params=pltpu.CompilerParams(collective_id=0, has_side_effects=True, vmem_limit_bytes=67043328),
         name='tail',
@@ -739,7 +749,7 @@
       *[g.reshape(-1, 128) for g in gains], rowmask.reshape(1, batch), gates,
       xvalid.reshape(4, bl, ntok), k_cross.reshape(4, bl, ntok, hd), v_cross.reshape(4, bl, ntok, hd),
       wo, wg, wu, wd, cq, cwo, cg, cu, cd)
-    return out.reshape(batch, dim)
+    return out.reshape(batch, dim).astype(bf16)
 
 
 def solution(mesh):

time: 114 us -> 113 us (level)
  other arithmetic: 0 us -> 3.25 us
  local copies, waits for them, and re-layouts: 2.65 us -> 0 us
  Pallas kernels: 111 us -> 109 us
    convert_element_type x0 -> x1, other arithmetic: none -> 3.25 us  [tail(): return out.reshape(batch, dim).astype(bf16)]
    unnamed x1 -> x0, local copies, waits for them, and re-layouts: 2.65 us -> none
    pallas_call x1, Pallas kernels: 97.6 us -> 96.1 us  [tail(): pl.pallas_call(functools.partial(tail_kernel, (heads, hd, dim, mlp, ntok)...]
where the time goes in v5:
time: 113 us
  Pallas kernels  109 us (96%)
  other arithmetic  3.25 us (3%)
    pallas_call x1, Pallas kernels, tail(): pl.pallas_call(functools.partial(tail_kernel, (heads, hd, dim, mlp, ntok)...  96.1 us
    pallas_call x1, Pallas kernels, front(): pl.pallas_call(functools.partial(front_kernel, (heads, hd, dim, batch, sl...  12.5 us
    convert_element_type x1, other arithmetic, tail(): return out.reshape(batch, dim).astype(bf16)  3.25 us

profile of v5, /device:TPU:97, one launch (start us, length us, event | category | flops | bytes accessed | tf_op | source)
XLA Modules:
  0.0 112.5 jit_solution(11955522655788073311)
XLA Ops:
  0.6 12.5 %front.1 = (bf16[256,64,128]{2,1,0:T(8,128)(2,1)}, bf16[256,64,128]{2,1,0:T(8,128)(2,1)}, f32[256,512]{1,0:T(8,128)}) custom-call(bf16[256,3072]{1,0:T(8,128)(2,1)} %hid_h.1, s32[1,256]{1,0:T(1,128)} %bitcast.33, s32[256]{0:T(256)} %pos_s.1, bf16[24,128]{1,0:T(8,128)(2,1)} %bitcast.29, f32[1,128]{1,0:T(1,128)} %constant.2.clone.freq_v, ...), custom_call_target="tpu_custom_call" | custom-call | tf_op jit(solution)/shard_map/front/pallas_call | solution.py:192
  13.1 96.1 %tail.1 = f32[4,2,4,8,3072]{4,3,2,1,0:T(8,128)} custom-call(f32[4,2,32,512]{3,2,1,0:T(8,128)} %bitcast.28, bf16[8,4,8,3072]{3,2,1,0:T(8,128)(2,1)} %bitcast.23, bf16[24,128]{1,0:T(8,128)(2,1)} %bitcast.30, bf16[24,128]{1,0:T(8,128)(2,1)} %bitcast.31, bf16[24,128]{1,0:T(8,128)(2,1)} %bitcast.32, bf16[1,128]{1,0:T(2,128)(2,1)} %bitcast.35, s32[1,256]{1,0:T(1,128)} %bitcast.34, ...), custom_call_target="tpu_custom_call" | custom-call | tf_op jit(solution)/shard_map/tail/pallas_call | solution.py:740
  109.3 3.2 %convert_element_type.6 = bf16[4,2,4,8,3072]{4,3,2,1,0:T(8,128)(2,1)} convert(f32[4,2,4,8,3072]{4,3,2,1,0:T(8,128)} %tail.1) | non-fusion elementwise | flops 786432 | bytes 4718592 | tf_op jit(solution)/shard_map/convert_element_type | solution.py:752

commit v6 on v5

--- a/solution.py
+++ b/solution.py
@@ -33,14 +33,13 @@
     return jnp.dot(a, b, preferred_element_type=jnp.float32)
 
 
-def front_kernel(cfg, hid_h, posr_v, pos_s, gain_v, freq_v, wq_h, wk_h, wv_h, k_h, v_h, ko_h, vo_h, blk_v,
-                 hid_v, xn, wq_v, wkv_v, kc, vc, q3, o3, st3, kn, vn, in_sem, kv_sem, out_sem):
+def front_kernel(cfg, hid_h, posr_v, pos_s, gain_v, freq_v, wq_h, wk_h, wv_h, k_h, v_h, ko_h, vo_h, q_h,
+                 hid_v, xn, wq_v, wkv_v, kc, vc, q3, kn, vn, in_sem, kv_sem, out_sem):
     heads, hd, dim, batch, slots = cfg
     f32, bf16 = jnp.float32, jnp.bfloat16
-    per = 64
+    per = 32
     nch = batch // per
     nrm = 32
-    scale = hd ** -0.5
     first_slot = lax.axis_index('sp') * slots
 
     def loop(n, body):
@@ -110,19 +109,15 @@
     kv = fdot(xn[...], wkv_v[...])
     kn[...] = rope(kv[:, :hd])
     vn[...] = kv[:, hd:].astype(bf16).astype(f32)
-
-    lane = lax.broadcasted_iota(jnp.int32, (8, 128), 1)
-    sub = lax.broadcasted_iota(jnp.int32, (8, 128), 0)
+    q_cp = pltpu.make_async_copy(q3, q_h, in_sem.at[3 + batch // nrm])
+    q_cp.start()
     row16 = lax.broadcasted_iota(jnp.int32, (16, hd), 0)
-    zero = jnp.zeros((8, 128), f32)
-
-    def attend(g):
+
+    def patch(g):
         wait_both(ld_kv(g))
-        lps = []
         for i in range(per):
             b = g * per + i
             lp = pos_s[b] - first_slot
-            lps.append(lp)
             base = pl.multiple_of(lax.shift_left(lax.shift_right_logical(jnp.clip(lp, 0, slots - 1), 4), 4), 16)
             hit = row16 + base == lp
             for ref, new in ((kc, kn), (vc, vn)):
@@ -130,52 +125,9 @@
                 fresh = jnp.broadcast_to(new[pl.ds(b, 1), :], (16, hd))
                 ref[b, pl.ds(base, 16), :] = jnp.where(hit, fresh, old).astype(bf16)
         start_both(st_kv(g))
-        fours = [pl.ds(g * per + 4 * t, 4) for t in range(per // 4)]
-
-        def scores(ts):
-            return [lax.dot_general(q3[fours[t]].reshape(32, hd).astype(bf16), kc[fours[t]].reshape(4 * slots, hd),
-                                    (((1,), (1,)), ((), ())), preferred_element_type=f32) * scale for t in ts]
-
-        def soften(ts, sgs):
-            out = []
-            for t, sg in zip(ts, sgs):
-                probs, stats = [], []
-                for i in range(4):
-                    off = slots * (i % 2)
-                    lp = jnp.minimum(lps[4 * t + i], slots - 1)
-                    seen = (lane >= off) & (lane <= off + lp)
-                    sc = jnp.where(seen, sg[8 * i:8 * i + 8, 128 * (i // 2):128 * (i // 2) + 128], NEG_BIG)
-                    mx = jnp.max(sc, axis=1, keepdims=True)
-                    pr = jnp.where(seen, jnp.exp(sc - mx), 0.0)
-                    ls = jnp.sum(pr, axis=1, keepdims=True)
-                    stats.append(jnp.where(lane == sub, mx, jnp.where(lane == sub + 8, ls, 0.0)))
-                    probs.append(jnp.concatenate([pr, zero] if i < 2 else [zero, pr], axis=1))
-                out.append((jnp.concatenate(probs, axis=0).astype(bf16), stats))
-            return out
-
-        def mix(ts, prs):
-            return [fdot(pg, vc[fours[t]].reshape(4 * slots, hd)) for t, (pg, _) in zip(ts, prs)]
-
-        sets = [range(t, t + 4) for t in range(0, per // 4, 4)]
-        raw, soft, mixed = [scores(sets[0])], [], []
-        for k, ts in enumerate(sets):
-            if k + 1 < len(sets):
-                raw.append(scores(sets[k + 1]))
-            soft.append(soften(ts, raw[k]))
-            mixed += mix(ts, soft[k])
-        flat = [st for sf in soft for _, st in sf]
-        for t, (o, stats) in enumerate(zip(mixed, flat)):
-            o3[fours[t]] = o.reshape(4, 8, hd)
-            for i in range(4):
-                st3[g * per + 4 * t + i] = stats[i]
-
-    loop(nch, attend)
-    stat = st3[:, 0, :]
-    for h in range(1, heads):
-        stat = stat + st3[:, h, :]
-    for h in range(heads):
-        blk_v[:, h * hd:(h + 1) * hd] = o3[:, h, :]
-    blk_v[:, heads * hd:] = stat
+
+    loop(nch, patch)
+    q_cp.wait()
     loop(nch, lambda g: wait_both(st_kv(g)))
 
 
@@ -187,13 +139,13 @@
     vmem = pl.BlockSpec(memory_space=pltpu.VMEM)
     smem = pl.BlockSpec(memory_space=pltpu.SMEM)
     dma = pltpu.SemaphoreType.DMA
-    nch = batch // 64
+    nch = batch // 32
     cache = jax.ShapeDtypeStruct((batch, slots, hd), bf16)
-    ko, vo, blk = pl.pallas_call(
+    ko, vo, q = pl.pallas_call(
         functools.partial(front_kernel, (heads, hd, dim, batch, slots)),
-        out_shape=(cache, cache, jax.ShapeDtypeStruct((batch, heads * hd + hd), f32)),
+        out_shape=(cache, cache, jax.ShapeDtypeStruct((batch, 8, hd), f32)),
         in_specs=[anyspec, vmem, smem, vmem, vmem] + [anyspec] * 5,
-        out_specs=(anyspec, anyspec, vmem),
+        out_specs=(anyspec, anyspec, anyspec),
         scratch_shapes=[
             pltpu.VMEM((batch, dim), bf16),
             pltpu.VMEM((batch, dim), bf16),
@@ -202,11 +154,9 @@
             pltpu.VMEM((batch, slots, hd), bf16),
             pltpu.VMEM((batch, slots, hd), bf16),
             pltpu.VMEM((batch, 8, hd), f32),
-            pltpu.VMEM((batch, 8, hd), f32),
-            pltpu.VMEM((batch, 8, hd), f32),
             pltpu.VMEM((batch, hd), f32),
             pltpu.VMEM((batch, hd), f32),
-            dma((3 + batch // 32,)),
+            dma((4 + batch // 32,)),
             dma((2, nch)),
             dma((2, nch)),
         ],
@@ -214,16 +164,18 @@
         name='front',
     )(hidden, new_pos.reshape(1, batch), new_pos, gain.reshape(dim // 128, 128), jnp.asarray(rope_freqs(hd)),
       wq, wk, wv, k_self.reshape(batch, slots, hd), v_self.reshape(batch, slots, hd))
-    return ko.reshape(k_self.shape), vo.reshape(v_self.shape), blk
-
-
-def tail_kernel(cfg, blk_h, hid_h, g2_v, g3_v, g4_v, qn_v, rowm_v, gate_s, xv_h, kc_h, vc_h,
+    return ko, vo, q
+
+
+def tail_kernel(cfg, q_h, ks_h, vs_h, pos_s, hid_h, g2_v, g3_v, g4_v, qn_v, rowm_v, gate_s, xv_h, kc_h, vc_h,
                 wo_h, wg_h, wu_h, wd_h, cq_h, cwo_h, cg_h, cu_h, cd_h, out_h,
-                bk, yr, yd, yt, yf, ob, hrow, hst,
+                qs_v, o3, st3, bk, yr, yd, yt, yf, ob, hrow, hst,
                 wo_v, wg_v, wu_v, wd_v, cq_v, cwo_v, kc_v, vc_v, xv_v,
                 pbuf, dbuf, s0, s1, r1, r2, xa, og, acc, act, q3, oc, fac,
-                ld_sem, w_sem, kv_sem, ys, yrs, pr_s, pr_r, ar_s, ar_r, lr_s, lr_r, xs_s, xs_r, fg_s, fg_r, out_sem):
-    heads, hd, dim, mlp, ntok = cfg
+                ld_sem, self_sem, w_sem, kv_sem, ys, yrs, pr_s, pr_r, ar_s, ar_r, lr_s, lr_r, xs_s, xs_r, fg_s, fg_r, out_sem):
+    heads, hd, dim, mlp, ntok, slots = cfg
+    per = ntok // slots
+    free = ks_h.shape[0] * ks_h.shape[1] // per // 8
     cw = dim // NC
     hw = heads * hd
     half = 32
@@ -255,7 +207,13 @@
             return carry
         lax.fori_loop(0, n, step, 0)
 
-    blk_cp = pltpu.make_async_copy(blk_h, bk, ld_sem.at[0])
+    def ld_self(t):
+        dest = ring(y + 2 + t - (t // 2) * (2 * t - 1))
+        span = pl.ds(t * 2 * half, 2 * half)
+        return (pltpu.make_async_copy(q_h.at[dest], qs_v.at[t], self_sem.at[0, t]),
+                pltpu.make_async_copy(ks_h.at[dest], kc_v.at[span], self_sem.at[1, t]),
+                pltpu.make_async_copy(vs_h.at[dest], vc_v.at[span], self_sem.at[2, t]))
+
     hid_cp = pltpu.make_async_copy(hid_h.at[y * 2 + c], hrow, ld_sem.at[1])
     xv_cp = pltpu.make_async_copy(xv_h.at[y], xv_v, ld_sem.at[2])
 
@@ -293,34 +251,38 @@
         return cols(cd_h, wd_v, 8, j)
 
     def ld_kc(g):
-        return pltpu.make_async_copy(kc_h.at[y, pl.ds(g * 8, 8)], kc_v.at[pl.ds(g * 8, 8)], kv_sem.at[0, g])
+        return pltpu.make_async_copy(kc_h.at[y, pl.ds(g * 8 * per, 8 * per)], kc_v.at[pl.ds(g * 8 * per, 8 * per)], kv_sem.at[0, g])
 
     def ld_vc(g):
-        return pltpu.make_async_copy(vc_h.at[y, pl.ds(g * 8, 8)], vc_v.at[pl.ds(g * 8, 8)], kv_sem.at[1, g])
-
-    blk_cp.start()
+        return pltpu.make_async_copy(vc_h.at[y, pl.ds(g * 8 * per, 8 * per)], vc_v.at[pl.ds(g * 8 * per, 8 * per)], kv_sem.at[1, g])
+
+    def start_self(t):
+        for cp in ld_self(t):
+            cp.start()
+
+    loop(4, start_self)
+    barrier = pltpu.get_barrier_semaphore()
+    for dev in (sib, xdev(1), xdev(2), xdev(-1), ydev(1), ydev(2), ydev(-1)):
+        pl.semaphore_signal(barrier, inc=1, device_id=dev, device_id_type=MESH)
     hid_cp.start()
     xv_cp.start()
     loop(NC, lambda j: ld_wo(j).start())
 
-    barrier = pltpu.get_barrier_semaphore()
-    for dev in (sib, xdev(1), xdev(2), xdev(-1), ydev(1), ydev(2), ydev(-1)):
-        pl.semaphore_signal(barrier, inc=1, device_id=dev, device_id_type=MESH)
-
     def start_gu(j):
         ld_wg(j).start()
         ld_wu(j).start()
 
-    loop(NC, start_gu)
-    loop(NC, lambda j: ld_wd(j).start())
-    loop(NC, lambda j: ld_cq(j).start())
-
     def start_kv(g):
         ld_kc(g).start()
         ld_vc(g).start()
 
-    loop(8, start_kv)
-    loop(NC, lambda j: ld_cwo(j).start())
+    def start_bulk():
+        loop(NC, start_gu)
+        loop(NC, lambda j: ld_wd(j).start())
+        loop(NC, lambda j: ld_cq(j).start())
+        loop(8 - free, lambda g: start_kv(g + free))
+        loop(NC, lambda j: ld_cwo(j).start())
+
     q3[...] = jnp.zeros_like(q3)
     nrow = rowm_v.shape[1]
     mine = (y * 2 + c) * half + lax.broadcasted_iota(jnp.int32, (half, nrow), 0)
@@ -357,11 +319,78 @@
     def y_final(j, d):
         return rcopy(yt.at[j], yf.at[j], ys.at[2, j], yrs.at[2, j], ydev(d))
 
-    blk_cp.wait()
-    for j, d in ((0, 1), (1, -1)):
-        y_relay(j, d).start()
-    for j, d in ((0, 1), (1, -1)):
-        y_direct(j, d).start()
+    lane8 = lax.broadcasted_iota(jnp.int32, (8, 128), 1)
+    sub8 = lax.broadcasted_iota(jnp.int32, (8, 128), 0)
+    zero8 = jnp.zeros((8, 128), jnp.float32)
+    nseq = 2 * half
+
+    def attend_self(t):
+        for cp in ld_self(t):
+            cp.wait()
+        dest = ring(y + 2 + t - (t // 2) * (2 * t - 1))
+        lps = [jnp.minimum(pos_s[dest * nseq + i] - y * slots, slots - 1) for i in range(nseq)]
+
+        def rows4(ref, u):
+            return ref[pl.ds(t * nseq + 4 * u, 4)].reshape(4 * slots, hd)
+
+        def scores(us):
+            return [lax.dot_general(qs_v[t, 4 * u:4 * u + 4].reshape(32, hd).astype(jnp.bfloat16), rows4(kc_v, u),
+                                    (((1,), (1,)), ((), ())), preferred_element_type=jnp.float32) * scale for u in us]
+
+        def soften(us, sgs):
+            out = []
+            for u, sg in zip(us, sgs):
+                probs, stats = [], []
+                for i in range(4):
+                    off = slots * (i % 2)
+                    seen = (lane8 >= off) & (lane8 <= off + lps[4 * u + i])
+                    sc = jnp.where(seen, sg[8 * i:8 * i + 8, 128 * (i // 2):128 * (i // 2) + 128], NEG_BIG)
+                    mx = jnp.max(sc, axis=1, keepdims=True)
+                    pr = jnp.where(seen, jnp.exp(sc - mx), 0.0)
+                    ls = jnp.sum(pr, axis=1, keepdims=True)
+                    stats.append(jnp.where(lane8 == sub8, mx, jnp.where(lane8 == sub8 + 8, ls, 0.0)))
+                    probs.append(jnp.concatenate([pr, zero8] if i < 2 else [zero8, pr], axis=1))
+                out.append((jnp.concatenate(probs, axis=0).astype(jnp.bfloat16), stats))
+            return out
+
+        def mix(us, prs):
+            return [fdot(pg, rows4(vc_v, u)) for u, (pg, _) in zip(us, prs)]
+
+        sets = [range(u, u + 4) for u in range(0, nseq // 4, 4)]
+        raw, soft, mixed = [scores(sets[0])], [], []
+        for k, us in enumerate(sets):
+            if k + 1 < len(sets):
+                raw.append(scores(sets[k + 1]))
+            soft.append(soften(us, raw[k]))
+            mixed += mix(us, soft[k])
+        flat = [st for sf in soft for _, st in sf]
+        for u, (o, stats) in enumerate(zip(mixed, flat)):
+            o3[4 * u:4 * u + 4] = o.reshape(4, 8, hd)
+            for i in range(4):
+                st3[4 * u + i] = stats[i]
+        stat = st3[:, 0, :]
+        for h in range(1, heads):
+            stat = stat + st3[:, h, :]
+        for h in range(heads):
+            bk[dest, :, :, h * hd:(h + 1) * hd] = o3[:, h, :].reshape(2, half, hd)
+        bk[dest, :, :, hw:] = stat.reshape(2, half, hd)
+
+        @pl.when(t == 0)
+        def _():
+            y_relay(0, 1).start()
+            y_relay(1, -1).start()
+            start_bulk()
+
+        @pl.when(t == 1)
+        def _():
+            y_direct(0, 1).start()
+
+        @pl.when(t == 2)
+        def _():
+            y_direct(1, -1).start()
+
+    loop(4, attend_self)
+    loop(free, start_kv)
     for j, d in ((0, 1), (1, -1)):
         y_relay(j, d).wait_recv()
         yt[j] = merge(bk[ring(y + d), j], yr[j])[0]
@@ -544,13 +573,16 @@
 
     nat = 16
 
+    def whole(ref, b):
+        return ref[pl.ds(b * per, per)].reshape(ntok, hd)
+
     def attend(t):
         for u in range(nat // 8):
             ld_kc(t * (nat // 8) + u).wait()
             ld_vc(t * (nat // 8) + u).wait()
 
         def scores(us):
-            return [lax.dot_general(q3[t * nat + u].astype(jnp.bfloat16), kc_v[t * nat + u], (((1,), (1,)), ((), ())),
+            return [lax.dot_general(q3[t * nat + u].astype(jnp.bfloat16), whole(kc_v, t * nat + u), (((1,), (1,)), ((), ())),
                                     preferred_element_type=jnp.float32) * scale for u in us]
 
         def soften(us, scs):
@@ -564,7 +596,7 @@
             return out
 
         def mix(us, prs):
-            return [fdot(pr, vc_v[t * nat + u]) / ls for u, (pr, ls) in zip(us, prs)]
+            return [fdot(pr, whole(vc_v, t * nat + u)) / ls for u, (pr, ls) in zip(us, prs)]
 
         xvs = [xv_v[pl.ds(pl.multiple_of(t * nat + 8 * u, 8), 8), :] for u in range(nat // 8)]
         one, two = range(nat // 2), range(nat // 2, nat)
@@ -676,10 +708,11 @@
         result_cp(j, 1).wait()
 
 
-def tail(blk, hidden, gains, rowmask, gates, xvalid, k_cross, v_cross, wo, wg, wu, wd, cq, cwo, cg, cu, cd, heads, hd):
+def tail(q, ko, vo, new_pos, hidden, gains, rowmask, gates, xvalid, k_cross, v_cross, wo, wg, wu, wd, cq, cwo, cg, cu, cd, heads, hd):
     batch, dim = hidden.shape
     mlp = wg.shape[1]
     ntok = xvalid.shape[1]
+    slots = ko.shape[1]
     cw = dim // NC
     hw = heads * hd
     bl = batch // 4
@@ -690,6 +723,9 @@
     smem = pl.BlockSpec(memory_space=pltpu.SMEM)
     dma = pltpu.SemaphoreType.DMA
     scratch = [
+        pltpu.VMEM((4, bl, 8, hd), f32),
+        pltpu.VMEM((bl, 8, hd), f32),
+        pltpu.VMEM((bl, 8, hd), f32),
         pltpu.VMEM((4, 2, half, hw + hd), f32),
         pltpu.VMEM((2, half, hw + hd), f32),
         pltpu.VMEM((2, half, hw + hd), f32),
@@ -704,8 +740,8 @@
         pltpu.VMEM((NC, mlp, cw), bf16),
         pltpu.VMEM((NC, cw, hw), bf16),
         pltpu.VMEM((NC, hw, cw), bf16),
-        pltpu.VMEM((bl, ntok, hd), bf16),
-        pltpu.VMEM((bl, ntok, hd), bf16),
+        pltpu.VMEM((bl * ntok // slots, slots, hd), bf16),
+        pltpu.VMEM((bl * ntok // slots, slots, hd), bf16),
         pltpu.VMEM((bl, ntok), jnp.int32),
         pltpu.VMEM((NC, 2, half, cw), f32),
         pltpu.VMEM((NC, half, cw), f32),
@@ -721,6 +757,7 @@
         pltpu.VMEM((bl, 8, hd), f32),
         pltpu.VMEM((2, 4, 8, 128), f32),
         dma((3,)),
+        dma((3, 4)),
         dma((9, NC)),
         dma((2, 8)),
         dma((3, 2)),
@@ -738,16 +775,16 @@
         dma((2, NC)),
     ]
     out = pl.pallas_call(
-        functools.partial(tail_kernel, (heads, hd, dim, mlp, ntok)),
+        functools.partial(tail_kernel, (heads, hd, dim, mlp, ntok, slots)),
         out_shape=jax.ShapeDtypeStruct((4, 2, 4, 8, dim), f32),
-        in_specs=[anyspec, anyspec] + [vmem] * 5 + [smem] + [anyspec] * 12,
+        in_specs=[anyspec] * 3 + [smem, anyspec] + [vmem] * 5 + [smem] + [anyspec] * 12,
         out_specs=anyspec,
         scratch_shapes=scratch,
         compiler_params=pltpu.CompilerParams(collective_id=0, has_side_effects=True, vmem_limit_bytes=67043328),
         name='tail',
-    )(blk.reshape(4, 2, half, hw + hd), hidden.reshape(8, 4, 8, dim),
+    )(q.reshape(4, bl, 8, hd), ko.reshape(4, bl, slots, hd), vo.reshape(4, bl, slots, hd), new_pos, hidden.reshape(8, 4, 8, dim),
       *[g.reshape(-1, 128) for g in gains], rowmask.reshape(1, batch), gates,
-      xvalid.reshape(4, bl, ntok), k_cross.reshape(4, bl, ntok, hd), v_cross.reshape(4, bl, ntok, hd),
+      xvalid.reshape(4, bl, ntok), k_cross.reshape(4, bl * ntok // slots, slots, hd), v_cross.reshape(4, bl * ntok // slots, slots, hd),
       wo, wg, wu, wd, cq, cwo, cg, cu, cd)
     return out.reshape(batch, dim).astype(bf16)
 
@@ -771,11 +808,11 @@
                    cross_wo, cross_gates, cross_mlp_norm, cross_wgate, cross_wup, cross_wdown):
         head_dim = k_self.shape[3]
         heads_local = self_wq.shape[1] // head_dim
-        k_new_cache, v_new_cache, blk = front(hidden, new_pos, k_self, v_self, self_attn_norm, self_wq, self_wk, self_wv,
-                                              heads_local, head_dim)
+        ko, vo, q = front(hidden, new_pos, k_self, v_self, self_attn_norm, self_wq, self_wk, self_wv,
+                          heads_local, head_dim)
         gains = (self_mlp_norm, cross_attn_norm, cross_mlp_norm, cross_qnorm)
-        h4 = tail(blk, hidden, gains, rowmask, cross_gates, xvalid, k_cross, v_cross, self_wo, self_wgate, self_wup, self_wdown,
+        h4 = tail(q, ko, vo, new_pos, hidden, gains, rowmask, cross_gates, xvalid, k_cross, v_cross, self_wo, self_wgate, self_wup, self_wdown,
                   cross_wq, cross_wo, cross_wgate, cross_wup, cross_wdown, heads_local, head_dim)
-        return h4, k_new_cache, v_new_cache
+        return h4, ko.reshape(k_self.shape), vo.reshape(v_self.shape)
 
     return jax.shard_map(local_step, mesh=mesh, in_specs=in_specs, out_specs=out_specs, check_vma=False)

time: 113 us -> 110 us (0.973)
  Pallas kernels: 109 us -> 106 us
    pallas_call x1, Pallas kernels: 12.5 us -> 9.1 us  [front(): pl.pallas_call(functools.partial(front_kernel, (heads, hd, dim, batch, sl...]
where the time goes in v6:
time: 110 us
  Pallas kernels  106 us (96%)
  other arithmetic  3.25 us (3%)
    pallas_call x1, Pallas kernels, tail(): pl.pallas_call(functools.partial(tail_kernel, (heads, hd, dim, mlp, ntok,...  96.7 us
    pallas_call x1, Pallas kernels, front(): pl.pallas_call(functools.partial(front_kernel, (heads, hd, dim, batch, sl...  9.1 us
    convert_element_type x1, other arithmetic, tail(): return out.reshape(batch, dim).astype(bf16)  3.25 us

profile of v6, /device:TPU:97, one launch (start us, length us, event | category | flops | bytes accessed | tf_op | source)
XLA Modules:
  0.0 109.7 jit_solution(893430335474657445)
XLA Ops:
  0.6 9.1 %front.1 = (bf16[256,64,128]{2,1,0:T(8,128)(2,1)}, bf16[256,64,128]{2,1,0:T(8,128)(2,1)}, f32[256,8,128]{2,1,0:T(8,128)}) custom-call(bf16[256,3072]{1,0:T(8,128)(2,1)} %hid_h.1, s32[1,256]{1,0:T(1,128)} %bitcast.35, s32[256]{0:T(256)} %pos_s.3, bf16[24,128]{1,0:T(8,128)(2,1)} %bitcast.36, f32[1,128]{1,0:T(1,128)} %constant.2.clone.freq_v, ...), custom_call_target="tpu_custom_call" | custom-call | tf_op jit(solution)/shard_map/front/pallas_call | solution.py:144
  9.7 96.7 %tail.1 = f32[4,2,4,8,3072]{4,3,2,1,0:T(8,128)} custom-call(f32[4,64,8,128]{3,2,1,0:T(8,128)} %bitcast.33, bf16[4,64,64,128]{3,2,1,0:T(8,128)(2,1)} %bitcast.26, bf16[4,64,64,128]{3,2,1,0:T(8,128)(2,1)} %bitcast.28, s32[256]{0:T(256)} %pos_s.3, bf16[8,4,8,3072]{3,2,1,0:T(8,128)(2,1)} %bitcast.25, bf16[24,128]{1,0:T(8,128)(2,1)} %bitcast.37, ...), custom_call_target="tpu_custom_call" | custom-call | tf_op jit(solution)/shard_map/tail/pallas_call | solution.py:777
  106.5 3.2 %convert_element_type.6 = bf16[4,2,4,8,3072]{4,3,2,1,0:T(8,128)(2,1)} convert(f32[4,2,4,8,3072]{4,3,2,1,0:T(8,128)} %tail.1) | non-fusion elementwise | flops 786432 | bytes 4718592 | tf_op jit(solution)/shard_map/convert_element_type | solution.py:789

commit v7 on v6

--- a/solution.py
+++ b/solution.py
@@ -168,11 +168,11 @@
 
 
 def tail_kernel(cfg, q_h, ks_h, vs_h, pos_s, hid_h, g2_v, g3_v, g4_v, qn_v, rowm_v, gate_s, xv_h, kc_h, vc_h,
-                wo_h, wg_h, wu_h, wd_h, cq_h, cwo_h, cg_h, cu_h, cd_h, out_h,
+                wo_h, wg_h, wu_h, wd_h, cq_h, cwo_h, cg_h, cu_h, cd_h, out_v,
                 qs_v, o3, st3, bk, yr, yd, yt, yf, ob, hrow, hst,
                 wo_v, wg_v, wu_v, wd_v, cq_v, cwo_v, kc_v, vc_v, xv_v,
                 pbuf, dbuf, s0, s1, r1, r2, xa, og, acc, act, q3, oc, fac,
-                ld_sem, self_sem, w_sem, kv_sem, ys, yrs, pr_s, pr_r, ar_s, ar_r, lr_s, lr_r, xs_s, xs_r, fg_s, fg_r, out_sem):
+                ld_sem, self_sem, w_sem, kv_sem, ys, yrs, pr_s, pr_r, ar_s, ar_r, lr_s, lr_r, xs_s, xs_r, fg_s, fg_r):
     heads, hd, dim, mlp, ntok, slots = cfg
     per = ntok // slots
     free = ks_h.shape[0] * ks_h.shape[1] // per // 8
@@ -295,20 +295,12 @@
     lane = lax.broadcasted_iota(jnp.int32, (half, hd), 1)
 
     def merge(a, b):
-        outs, ms, ls = [], [], []
-        for h in range(heads):
-            ma, mb = a[:, hw + h:hw + h + 1], b[:, hw + h:hw + h + 1]
-            la, lb = a[:, hw + 8 + h:hw + 9 + h], b[:, hw + 8 + h:hw + 9 + h]
-            mm = jnp.maximum(ma, mb)
-            ea, eb = jnp.exp(ma - mm), jnp.exp(mb - mm)
-            outs.append(a[:, h * hd:(h + 1) * hd] * ea + b[:, h * hd:(h + 1) * hd] * eb)
-            ms.append(mm)
-            ls.append(la * ea + lb * eb)
-        stat = jnp.zeros((half, hd), jnp.float32)
-        for h in range(heads):
-            stat = jnp.where(lane == h, ms[h], stat)
-            stat = jnp.where(lane == 8 + h, ls[h], stat)
-        return jnp.concatenate(outs + [stat], axis=1), ls
+        sa, sb = a[:, hw:], b[:, hw:]
+        mm = jnp.maximum(sa, sb)
+        ea, eb = jnp.exp(sa - mm), jnp.exp(sb - mm)
+        stat = jnp.where(lane < 8, mm, sa * pltpu.roll(ea, 8, 1) + sb * pltpu.roll(eb, 8, 1))
+        outs = [a[:, h * hd:(h + 1) * hd] * ea[:, h:h + 1] + b[:, h * hd:(h + 1) * hd] * eb[:, h:h + 1] for h in range(heads)]
+        return jnp.concatenate(outs + [stat], axis=1), [stat[:, 8 + h:9 + h] for h in range(heads)]
 
     def y_relay(j, d):
         return rcopy(bk.at[ring(y + 2), j], yr.at[j], ys.at[0, j], yrs.at[0, j], ydev(d))
@@ -673,18 +665,19 @@
         st['got'][1].wait_recv()
         st['pair'][2].start()
 
-    def result_cp(j, cc):
-        return pltpu.make_async_copy(og.at[j, cc], out_h.at[:, cc, :, :, j * cw:(j + 1) * cw], out_sem.at[cc, j])
+    def result(j, cc):
+        for yy in range(4):
+            out_v[yy * 8 + cc * 4:yy * 8 + cc * 4 + 4, :, j * cw:(j + 1) * cw] = og[j, cc, yy].astype(jnp.bfloat16)
 
     for j in order:
         st = plans[j][1]
         st['got'][2].wait_recv()
         st['pair'][3].start()
-        result_cp(j, c).start()
     for j in order:
         for cp in plans[j][1]['pair']:
             cp.wait_recv()
-        result_cp(j, 1 - c).start()
+        result(j, 0)
+        result(j, 1)
 
     for j, d in ((0, 1), (1, -1)):
         y_relay(j, d).wait_send()
@@ -703,9 +696,6 @@
         for st in plans[j]:
             for cp in st['own'] + st['relay'] + st['pair']:
                 cp.wait_send()
-    for j in order:
-        result_cp(j, 0).wait()
-        result_cp(j, 1).wait()
 
 
 def tail(q, ko, vo, new_pos, hidden, gains, rowmask, gates, xvalid, k_cross, v_cross, wo, wg, wu, wd, cq, cwo, cg, cu, cd, heads, hd):
@@ -772,21 +762,20 @@
         dma((NC,)),
         dma((NC, 3, 4)),
         dma((NC, 3, 4)),
-        dma((2, NC)),
     ]
     out = pl.pallas_call(
         functools.partial(tail_kernel, (heads, hd, dim, mlp, ntok, slots)),
-        out_shape=jax.ShapeDtypeStruct((4, 2, 4, 8, dim), f32),
+        out_shape=pltpu.VMEM((batch // 8, 8, dim), bf16),
         in_specs=[anyspec] * 3 + [smem, anyspec] + [vmem] * 5 + [smem] + [anyspec] * 12,
-        out_specs=anyspec,
+        out_specs=vmem,
         scratch_shapes=scratch,
-        compiler_params=pltpu.CompilerParams(collective_id=0, has_side_effects=True, vmem_limit_bytes=67043328),
+        compiler_params=pltpu.CompilerParams(collective_id=0, has_side_effects=True, vmem_limit_bytes=61000000),
         name='tail',
     )(q.reshape(4, bl, 8, hd), ko.reshape(4, bl, slots, hd), vo.reshape(4, bl, slots, hd), new_pos, hidden.reshape(8, 4, 8, dim),
       *[g.reshape(-1, 128) for g in gains], rowmask.reshape(1, batch), gates,
       xvalid.reshape(4, bl, ntok), k_cross.reshape(4, bl * ntok // slots, slots, hd), v_cross.reshape(4, bl * ntok // slots, slots, hd),
       wo, wg, wu, wd, cq, cwo, cg, cu, cd)
-    return out.reshape(batch, dim).astype(bf16)
+    return out.reshape(batch, dim)
 
 
 def solution(mesh):

time: 110 us -> 107 us (0.973)
  other arithmetic: 3.25 us -> 0 us
  local copies, waits for them, and re-layouts: 0 us -> 1.15 us
    convert_element_type x1 -> x0, other arithmetic: 3.25 us -> none  [tail(): return out.reshape(batch, dim).astype(bf16)]
    unnamed x0 -> x1, local copies, waits for them, and re-layouts: none -> 1.15 us
where the time goes in v7:
time: 107 us
  Pallas kernels  105 us (98%)
  local copies, waits for them, and re-layouts  1.15 us (1%)
    pallas_call x1, Pallas kernels, tail(): pl.pallas_call(functools.partial(tail_kernel, (heads, hd, dim, mlp, ntok,...  96 us
    pallas_call x1, Pallas kernels, front(): pl.pallas_call(functools.partial(front_kernel, (heads, hd, dim, batch, sl...  9.1 us

profile of v7, /device:TPU:97, one launch (start us, length us, event | category | flops | bytes accessed | tf_op | source)
XLA Modules:
  0.0 106.9 jit_solution(3909743826459437711)
XLA Ops:
  0.6 9.1 %front.1 = (bf16[256,64,128]{2,1,0:T(8,128)(2,1)}, bf16[256,64,128]{2,1,0:T(8,128)(2,1)}, f32[256,8,128]{2,1,0:T(8,128)}) custom-call(bf16[256,3072]{1,0:T(8,128)(2,1)} %hid_h.1, s32[1,256]{1,0:T(1,128)} %bitcast.35, s32[256]{0:T(256)} %pos_s.3, bf16[24,128]{1,0:T(8,128)(2,1)} %bitcast.36, f32[1,128]{1,0:T(1,128)} %constant.2.clone.freq_v, ...), custom_call_target="tpu_custom_call" | custom-call | tf_op jit(solution)/shard_map/front/pallas_call | solution.py:144
  9.7 96.0 %tail.1 = bf16[32,8,3072]{2,1,0:T(8,128)(2,1)S(1)} custom-call(f32[4,64,8,128]{3,2,1,0:T(8,128)} %bitcast.33, bf16[4,64,64,128]{3,2,1,0:T(8,128)(2,1)} %bitcast.27, bf16[4,64,64,128]{3,2,1,0:T(8,128)(2,1)} %bitcast.29, s32[256]{0:T(256)} %pos_s.3, bf16[8,4,8,3072]{3,2,1,0:T(8,128)(2,1)} %bitcast.26, bf16[24,128]{1,0:T(8,128)(2,1)} %bitcast.37, ...), custom_call_target="tpu_custom_call" | custom-call | tf_op jit(solution)/shard_map/tail/pallas_call | solution.py:766
  105.7 1.1 %copy.33 = bf16[256,3072]{1,0:T(8,128)(2,1)} copy(bf16[256,3072]{1,0:T(8,128)(2,1)S(1)} %bitcast.23) | data formatting | bytes 3145728

commit v8 on v7

--- a/solution.py
+++ b/solution.py
@@ -15,7 +15,7 @@
 HIGH_FREQ = 4.0
 ORIG_CTX = 8192.0
 NEG_BIG = -1e30
-NC = 6
+NC = 4
 MESH = pl.DeviceIdType.MESH
 
 
@@ -242,13 +242,13 @@
         return cols(cwo_h, cwo_v, 5, j)
 
     def ld_cg(j):
-        return rows(cg_h, wg_v, 6, j)
+        return rows(cg_h, wg_v, 1, j)
 
     def ld_cu(j):
-        return rows(cu_h, wu_v, 7, j)
+        return rows(cu_h, wu_v, 2, j)
 
     def ld_cd(j):
-        return cols(cd_h, wd_v, 8, j)
+        return cols(cd_h, wd_v, 3, j)
 
     def ld_kc(g):
         return pltpu.make_async_copy(kc_h.at[y, pl.ds(g * 8 * per, 8 * per)], kc_v.at[pl.ds(g * 8 * per, 8 * per)], kv_sem.at[0, g])
@@ -628,7 +628,7 @@
         return (lambda k: og.at[j, c, ring(y + k), x], ydev), (lambda k: og.at[j, c, :, ring(x + k)], xdev)
 
     def fg(j, stage, k, s, what, dev):
-        return rcopy(what, what, fg_s.at[j, stage, s], fg_r.at[j, stage, k], dev)
+        return rcopy(what, what, fg_s.at[j, 3 * stage + s], fg_r.at[j, 3 * stage + k], dev)
 
     plans = []
     for j in range(NC):
@@ -748,7 +748,7 @@
         pltpu.VMEM((2, 4, 8, 128), f32),
         dma((3,)),
         dma((3, 4)),
-        dma((9, NC)),
+        dma((6, NC)),
         dma((2, 8)),
         dma((3, 2)),
         dma((3, 2)),
@@ -760,8 +760,8 @@
         dma((3, NC)),
         dma((NC,)),
         dma((NC,)),
-        dma((NC, 3, 4)),
-        dma((NC, 3, 4)),
+        dma((NC, 10)),
+        dma((NC, 10)),
     ]
     out = pl.pallas_call(
         functools.partial(tail_kernel, (heads, hd, dim, mlp, ntok, slots)),

time: 107 us -> 106 us (level)
  no operation moved by 1% of the time
where the time goes in v8:
time: 106 us
  Pallas kernels  104 us (98%)
  local copies, waits for them, and re-layouts  1.15 us (1%)
    pallas_call x1, Pallas kernels, tail(): pl.pallas_call(functools.partial(tail_kernel, (heads, hd, dim, mlp, ntok,...  95.2 us
    pallas_call x1, Pallas kernels, front(): pl.pallas_call(functools.partial(front_kernel, (heads, hd, dim, batch, sl...  9.1 us

profile of v8, /device:TPU:97, one launch (start us, length us, event | category | flops | bytes accessed | tf_op | source)
XLA Modules:
  0.0 106.1 jit_solution(18039846371655529022)
XLA Ops:
  0.6 9.1 %front.1 = (bf16[256,64,128]{2,1,0:T(8,128)(2,1)}, bf16[256,64,128]{2,1,0:T(8,128)(2,1)}, f32[256,8,128]{2,1,0:T(8,128)}) custom-call(bf16[256,3072]{1,0:T(8,128)(2,1)} %hid_h.1, s32[1,256]{1,0:T(1,128)} %bitcast.35, s32[256]{0:T(256)} %pos_s.3, bf16[24,128]{1,0:T(8,128)(2,1)} %bitcast.36, f32[1,128]{1,0:T(1,128)} %constant.2.clone.freq_v, ...), custom_call_target="tpu_custom_call" | custom-call | tf_op jit(solution)/shard_map/front/pallas_call | solution.py:144
  9.7 95.2 %tail.1 = bf16[32,8,3072]{2,1,0:T(8,128)(2,1)S(1)} custom-call(f32[4,64,8,128]{3,2,1,0:T(8,128)} %bitcast.33, bf16[4,64,64,128]{3,2,1,0:T(8,128)(2,1)} %bitcast.27, bf16[4,64,64,128]{3,2,1,0:T(8,128)(2,1)} %bitcast.29, s32[256]{0:T(256)} %pos_s.3, bf16[8,4,8,3072]{3,2,1,0:T(8,128)(2,1)} %bitcast.26, bf16[24,128]{1,0:T(8,128)(2,1)} %bitcast.37, ...), custom_call_target="tpu_custom_call" | custom-call | tf_op jit(solution)/shard_map/tail/pallas_call | solution.py:766
  104.9 1.1 %copy.33 = bf16[256,3072]{1,0:T(8,128)(2,1)} copy(bf16[256,3072]{1,0:T(8,128)(2,1)S(1)} %bitcast.23) | data formatting | bytes 3145728
